TPU v7x, 128 devices: a whole 4x4x4 slice. The times are simulated.
128 devices in a mesh: row: 8 (over y, x_lo), col: 16 (over z, x_hi, core).
Axes of the slice: x: 4 (x_hi: 2, x_lo: 2; x = x_hi * 2 + x_lo), y: 4, z: 4, core: 2. Of those that a mesh axis runs over, the one named last changes fastest.
Arguments:
- gains: float32 [512, 8, 256], P(('row', 'col')), may hold values from -6 to 6
- coherency: bfloat16 [512, 512, 8, 1, 256], P('row', 'col'), may hold values from -6 to 6
- cotangent: bfloat16 [512, 512, 8, 1, 8], P('row', 'col'), may hold values from -0.099609375 to 0.099609375
- flags: int32 [512, 512, 1], P('row', 'col'), may hold values 0 or 1
- station_slot: int32 [512], replicated, may hold values from 0 to 511, as said below
Outputs:
- gain_grad: float32 [512, 8, 256], P(('row', 'col'))
Inputs may be any that keep to these rules, and one draw needn't show every extreme that they name: `station_slot`: each station appears in exactly one slot; in every aligned block of 4 consecutive slots the stations lie with 4 different holders, station s being held by the device of index s // 4 in the order of row+col.
All inputs are finite; a program needn't handle non-finite values. No bound on the sum of `flags` on one device may be relied on, other than what follows from the above.
Results may differ from a plain program's by a relative error of at most 0.0003.
Values sent between devices are 32-bit elements; how exact they have to be, the bound alone decides.
No kernel may reach another device: no remote copies, remote signals or barrier semaphores. Data moves between devices by JAX's collectives and lax.ppermute only.
A program may use at most 128 MiB of HBM per device.

v0:
```python
import jax
import jax.numpy as jnp
from jax import lax
from jax.sharding import PartitionSpec as P


def laid_out(blocks, dim):
    dims = list(blocks.shape[1:])
    dims[dim] *= blocks.shape[0]
    return jnp.moveaxis(blocks, 0, dim).reshape(dims)


def copy_for_each(x, axis):
    copies = jnp.broadcast_to(x, (lax.axis_size(axis), *x.shape))
    return lax.all_to_all(copies, axis, split_axis=0, concat_axis=0, tiled=True)


def gathered_copies(x, axis, dim):
    return laid_out(copy_for_each(x, axis), dim)


def split_up(x, dim, length):
    before, after = (x.shape[:dim], x.shape[dim + 1 :])
    return jnp.moveaxis(x.reshape(*before, length, -1, *after), dim, 0)


def summed_on_arrival(x, axis, dim):
    blocks = split_up(x, dim, lax.axis_size(axis))
    arrived = lax.all_to_all(blocks, axis, split_axis=0, concat_axis=0, tiled=True)
    return arrived.sum(axis=0)


def side_by_side(arrays, axis, split_dim, concat_dim, along):
    ends, at = ([], 0)
    for a in arrays[:-1]:
        at += a.shape[along]
        ends.append(at)
    both = jnp.concatenate(arrays, axis=along)
    return tuple(
        jnp.split(
            lax.all_to_all(both, axis, split_axis=split_dim, concat_axis=concat_dim, tiled=True),
            ends,
            axis=along,
        )
    )


def complex_product(first, second):
    return (
        first[0] * second[0] - first[1] * second[1],
        first[0] * second[1] + first[1] * second[0],
    )


def complex_sum(first, second):
    return (first[0] + second[0], first[1] + second[1])


def conjugate(element):
    return (element[0], -element[1])


def jones_product(first, second):
    return [
        complex_sum(
            complex_product(first[2 * row_index], second[column]),
            complex_product(first[2 * row_index + 1], second[2 + column]),
        )
        for row_index in (0, 1)
        for column in (0, 1)
    ]


def hermitian(matrix):
    return [conjugate(matrix[0]), conjugate(matrix[2]), conjugate(matrix[1]), conjugate(matrix[3])]


def as_complex(parts):
    return [(parts[0], parts[1]), (parts[2], parts[3]), (parts[4], parts[5]), (parts[6], parts[7])]


def as_parts(matrix):
    return [number for element in matrix for number in element]


def block_gradients(coherency, cotangent, flags, row_gains, col_gains):
    shape = coherency.shape
    directions = shape[4] // 8
    coherence = coherency.reshape(shape[:4] + (8, directions))
    weight = flags.astype(jnp.float32)[:, :, None, :, None]
    residual = as_complex(
        [
            cotangent[..., component].astype(jnp.float32)[..., None] * weight
            for component in range(8)
        ]
    )
    model_parts = as_complex(
        [coherence[..., component, :].astype(jnp.float32) for component in range(8)]
    )
    row_split = row_gains.reshape(row_gains.shape[0], row_gains.shape[1], 8, directions)
    col_split = col_gains.reshape(col_gains.shape[0], col_gains.shape[1], 8, directions)
    row_jones = as_complex([row_split[:, None, :, None, component, :] for component in range(8)])
    col_jones = as_complex([col_split[None, :, :, None, component, :] for component in range(8)])
    outgoing = jones_product(jones_product(residual, col_jones), hermitian(model_parts))
    row_side = jnp.stack([jnp.sum(part, axis=(1, 3)) for part in as_parts(outgoing)], axis=2)
    incoming = jones_product(jones_product(hermitian(residual), row_jones), model_parts)
    col_side = jnp.stack([jnp.sum(part, axis=(0, 3)) for part in as_parts(incoming)], axis=2)
    return (row_side.reshape(row_gains.shape), col_side.reshape(col_gains.shape))


def selector(identifiers, count):
    return (identifiers[:, None] == jnp.arange(count, dtype=jnp.int32)[None, :]).astype(jnp.float32)


def select_rows(table, values):
    return jnp.dot(
        table, values, precision=lax.Precision.HIGHEST, preferred_element_type=jnp.float32
    )


def shards(gains, coherency, cotangent, flags, station_slot):
    stations = station_slot.shape[0]
    share = gains.shape[0]
    flat = gains.shape[1] * gains.shape[2]
    row_total = lax.axis_size("row")
    col_total = lax.axis_size("col")
    groups = row_total * col_total
    row_place = lax.axis_index("row")
    col_place = lax.axis_index("col")
    device_place = row_place * col_total + col_place
    counting = jnp.arange(share, dtype=jnp.int32)
    slot_of = (
        jnp.zeros((stations,), jnp.int32)
        .at[station_slot]
        .set(jnp.arange(stations, dtype=jnp.int32))
    )
    own_blocks = jnp.take(slot_of, device_place * share + counting) // share
    col_target = own_blocks % row_total * col_total + own_blocks // row_total
    col_block = col_place * row_total + row_place
    row_holder = jnp.take(station_slot, device_place * share + counting) // share
    col_holder = jnp.take(station_slot, col_block * share + counting) // share
    row_count = coherency.shape[0]
    col_count = coherency.shape[1]
    row_ids = lax.dynamic_slice_in_dim(station_slot, row_place * row_count, row_count)
    col_ids = lax.dynamic_slice_in_dim(station_slot, col_place * col_count, col_count)
    col_piece = gathered_copies(gains, "col", 0)
    every_gain = lax.all_gather(col_piece, "row", axis=0, tiled=True)
    row_gains = jnp.take(every_gain, row_ids, axis=0)
    col_gains = jnp.take(every_gain, col_ids, axis=0)
    row_side, col_side = block_gradients(coherency, cotangent, flags, row_gains, col_gains)
    row_sum = summed_on_arrival(row_side, "col", 0)
    col_sum = summed_on_arrival(col_side, "row", 0)
    back_row = select_rows(selector(row_holder, groups).T, row_sum.reshape(share, flat))
    back_col = select_rows(selector(col_holder, groups).T, col_sum.reshape(share, flat))
    recv_row, recv_col = side_by_side((back_row, back_col), ("row", "col"), 0, 0, 1)
    result = select_rows(selector(own_blocks, groups), recv_row) + select_rows(
        selector(col_target, groups), recv_col
    )
    return result.reshape(gains.shape)


def solution(mesh):
    placed = (
        P(("row", "col"), None, None),
        P("row", "col", None, None, None),
        P("row", "col", None, None, None),
        P("row", "col", None),
        P(),
    )
    return jax.shard_map(
        shards, mesh=mesh, in_specs=placed, out_specs=P(("row", "col"), None, None), check_vma=False
    )
```

profile of v0, /device:TPU:1, one launch (start us, length us, event | category | flops | bytes accessed | tf_op | source)
XLA Modules:
  0.0 348.7 jit_solution(1977223666826343122)
XLA Ops:
  6.5 0.8 broadcast_in_dim.52
  7.3 20.3 %all_to_all.27 = f32[16,4,8,256]{3,2,1,0:T(8,128)} all-to-all(f32[16,4,8,256]{3,2,1,0:T(8,128)S(1)} %broadcast_in_dim.52), channel_id=1, replica_groups=mesh['row'=8,'col'=16] {'col'}, dimensions={0} | all-to-all | bytes 1048576 | tf_op jit(solution)/shard_map/all_to_all | solution.py:15
  27.7 0.7 convert_element_type.404
  28.5 17.5 %copy.42 = bf16[64,32,8,1,256]{0,4,2,1,3:T(8,128)(2,1)} copy(bf16[64,32,8,1,256]{4,2,3,1,0:T(8,128)(2,1)} %param.8) | data formatting | bytes 16777216 | tf_op args[1]
  46.0 0.6 gather_fusion.4
  46.8 1.4 fusion.93
  48.3 67.3 %all-gather.2.cloned.1.call-done = f32[512,8,256]{2,1,0:T(8,128)} async-done(((f32[64,8,256]{2,1,0:T(8,128)}), f32[512,8,256]{2,1,0:T(8,128)}) %all-gather.2.cloned.1.call-update) | async-done | bytes 4194320 | tf_op jit(solution)/shard_map/all_gather | solution.py:147
  115.5 2.8 gather_fusion.1
  118.3 0.4 copy.51
  118.9 8.5 %fusion.69 = f32[32,8,32]{2,1,0:T(8,128)S(1)} fusion(f32[64,8,32]{0,2,1:T(8,128)S(1)} %get-tuple-element.29, f32[64,8,32]{0,2,1:T(8,128)S(1)} %get-tuple-element.30, f32[64,8,32]{0,2,1:T(8,128)S(1)} %get-tuple-element.31, f32[64,8,32]{0,2,1:T(8,128)S(1)} %get-tuple-element.32, f32[64,8,32]{0,2,1:T(8,128)S(1)} %get-tuple-element.33, ...), kind=kLoop, calls=%fused_computation.127 | loop fusion | flops 20963328 | bytes 5013504 | tf_op jit(solution)/shard_map/reduce_sum | solution.py:107
  127.5 8.5 %fusion.66 = f32[32,8,32]{2,1,0:T(8,128)} fusion(f32[64,8,32]{0,2,1:T(8,128)S(1)} %get-tuple-element.29, f32[64,8,32]{0,2,1:T(8,128)S(1)} %get-tuple-element.30, f32[64,8,32]{0,2,1:T(8,128)S(1)} %get-tuple-element.31, f32[64,8,32]{0,2,1:T(8,128)S(1)} %get-tuple-element.32, f32[64,8,32]{0,2,1:T(8,128)S(1)} %get-tuple-element.33, ...), kind=kLoop, calls=%fused_computation.124 | loop fusion | flops 20963328 | bytes 5013504 | tf_op jit(solution)/shard_map/reduce_sum | solution.py:107
  136.0 6.9 %fusion.53 = f32[32,8,32]{2,1,0:T(8,128)} fusion(f32[64,8,32]{0,2,1:T(8,128)S(1)} %get-tuple-element.29, f32[64,8,32]{0,2,1:T(8,128)S(1)} %get-tuple-element.30, f32[64,8,32]{0,2,1:T(8,128)S(1)} %get-tuple-element.31, f32[64,8,32]{0,2,1:T(8,128)S(1)} %get-tuple-element.32, f32[64,8,32]{0,2,1:T(8,128)S(1)} %get-tuple-element.33, ...), kind=kLoop, calls=%fused_computation.111 | loop fusion | flops 20963328 | bytes 5013504 | tf_op jit(solution)/shard_map/reduce_sum | solution.py:107
  142.9 6.9 %fusion.50 = f32[32,8,32]{2,1,0:T(8,128)} fusion(f32[64,8,32]{0,2,1:T(8,128)S(1)} %get-tuple-element.29, f32[64,8,32]{0,2,1:T(8,128)S(1)} %get-tuple-element.30, f32[64,8,32]{0,2,1:T(8,128)S(1)} %get-tuple-element.31, f32[64,8,32]{0,2,1:T(8,128)S(1)} %get-tuple-element.32, f32[64,8,32]{0,2,1:T(8,128)S(1)} %get-tuple-element.33, ...), kind=kLoop, calls=%fused_computation.108 | loop fusion | flops 20963328 | bytes 5013504 | tf_op jit(solution)/shard_map/reduce_sum | solution.py:107
  149.8 3.4 gather_fusion
  153.2 1.2 gather.16
  154.6 0.7 fusion.97
  155.3 11.8 %fusion.39 = f32[64,8,32]{0,2,1:T(8,128)S(1)} fusion(f32[64,32,8]{0,2,1:T(8,128)S(1)} %bitcast.387, f32[64,32,8]{0,2,1:T(8,128)S(1)} %bitcast.284, f32[64,32,8]{0,2,1:T(8,128)S(1)} %bitcast.383, f32[64,32,8]{0,2,1:T(8,128)S(1)} %bitcast.296, f32[32,8,32]{2,1,0:T(8,128)S(1)} %bitcast.308, f32[32,8,32]{2,1,0:T(8,128)S(1)} %bitcast.316, ...), kind=kLoop, calls=%fused_computation.97 | loop fusion | flops 22003712 | bytes 4784128 | tf_op jit(solution)/shard_map/reduce_sum | solution.py:105
  167.2 11.8 %fusion.36 = f32[64,8,32]{0,2,1:T(8,128)S(1)} fusion(f32[64,32,8]{0,2,1:T(8,128)S(1)} %bitcast.388, f32[64,32,8]{0,2,1:T(8,128)S(1)} %bitcast.285, f32[64,32,8]{0,2,1:T(8,128)S(1)} %bitcast.384, f32[64,32,8]{0,2,1:T(8,128)S(1)} %bitcast.297, f32[32,8,32]{2,1,0:T(8,128)S(1)} %bitcast.309, f32[32,8,32]{2,1,0:T(8,128)S(1)} %bitcast.317, ...), kind=kLoop, calls=%fused_computation.94 | loop fusion | flops 22003712 | bytes 4784128 | tf_op jit(solution)/shard_map/reduce_sum | solution.py:105
  179.0 11.8 %fusion.27 = f32[64,8,32]{0,2,1:T(8,128)S(1)} fusion(f32[64,32,8]{0,2,1:T(8,128)S(1)} %bitcast.389, f32[64,32,8]{0,2,1:T(8,128)S(1)} %bitcast.286, f32[64,32,8]{0,2,1:T(8,128)S(1)} %bitcast.385, f32[64,32,8]{0,2,1:T(8,128)S(1)} %bitcast.298, f32[32,8,32]{2,1,0:T(8,128)S(1)} %bitcast.310, f32[32,8,32]{2,1,0:T(8,128)S(1)} %bitcast.318, ...), kind=kLoop, calls=%fused_computation.85 | loop fusion | flops 22003712 | bytes 4784128 | tf_op jit(solution)/shard_map/reduce_sum | solution.py:105
  190.9 10.1 %fusion.24 = f32[64,8,32]{0,2,1:T(8,128)S(1)} fusion(f32[64,32,8]{0,2,1:T(8,128)S(1)} %bitcast.390, f32[64,32,8]{0,2,1:T(8,128)S(1)} %bitcast.287, f32[64,32,8]{0,2,1:T(8,128)S(1)} %bitcast.386, f32[64,32,8]{0,2,1:T(8,128)S(1)} %bitcast.299, f32[32,8,32]{2,1,0:T(8,128)S(1)} %bitcast.311, f32[32,8,32]{2,1,0:T(8,128)S(1)} %bitcast.319, ...), kind=kLoop, calls=%fused_computation.82 | loop fusion | flops 22003712 | bytes 4784128 | tf_op jit(solution)/shard_map/reduce_sum | solution.py:105
  201.0 10.7 %fusion.33 = f32[64,8,32]{0,2,1:T(8,128)} fusion(f32[32,8,32]{2,1,0:T(8,128)S(1)} %bitcast.312, f32[32,8,32]{2,1,0:T(8,128)S(1)} %bitcast.320, f32[32,8,32]{2,1,0:T(8,128)S(1)} %bitcast.328, f32[32,8,32]{2,1,0:T(8,128)S(1)} %bitcast.336, f32[32,8,32]{2,1,0:T(8,128)S(1)} %bitcast.344, f32[64,32,8]{0,2,1:T(8,128)S(1)} %bitcast.367, ...), kind=kLoop, calls=%fused_computation.91 | loop fusion | flops 22003712 | bytes 4784128 | tf_op jit(solution)/shard_map/reduce_sum | solution.py:105
  211.7 9.9 %fusion.18 = f32[64,8,32]{0,2,1:T(8,128)S(1)} fusion(f32[32,8,32]{2,1,0:T(8,128)S(1)} %bitcast.313, f32[32,8,32]{2,1,0:T(8,128)S(1)} %bitcast.321, f32[32,8,32]{2,1,0:T(8,128)S(1)} %bitcast.329, f32[32,8,32]{2,1,0:T(8,128)S(1)} %bitcast.337, f32[32,8,32]{2,1,0:T(8,128)S(1)} %bitcast.345, f32[64,32,8]{0,2,1:T(8,128)S(1)} %bitcast.368, ...), kind=kLoop, calls=%fused_computation.76 | loop fusion | flops 22003712 | bytes 4784128 | tf_op jit(solution)/shard_map/reduce_sum | solution.py:105
  221.6 6.2 %fusion.56 = f32[32,8,32]{2,1,0:T(8,128)S(1)} fusion(f32[64,32,8]{0,2,1:T(8,128)S(1)} %bitcast.379, f32[64,32,8]{0,2,1:T(8,128)S(1)} %bitcast.375, f32[64,8,32]{0,2,1:T(8,128)S(1)} %get-tuple-element.29, f32[64,8,32]{0,2,1:T(8,128)S(1)} %get-tuple-element.30, f32[64,8,32]{0,2,1:T(8,128)S(1)} %get-tuple-element.31, f32[64,8,32]{0,2,1:T(8,128)S(1)} %get-tuple-element.32, ...), kind=kLoop, calls=%fused_computation.114 | loop fusion | flops 20963328 | bytes 5013504 | tf_op jit(solution)/shard_map/reduce_sum | solution.py:107
  227.8 6.2 %fusion.72 = f32[32,8,32]{2,1,0:T(8,128)S(1)} fusion(f32[64,32,8]{0,2,1:T(8,128)S(1)} %bitcast.380, f32[64,32,8]{0,2,1:T(8,128)S(1)} %bitcast.376, f32[64,8,32]{0,2,1:T(8,128)S(1)} %get-tuple-element.29, f32[64,8,32]{0,2,1:T(8,128)S(1)} %get-tuple-element.30, f32[64,8,32]{0,2,1:T(8,128)S(1)} %get-tuple-element.31, f32[64,8,32]{0,2,1:T(8,128)S(1)} %get-tuple-element.32, ...), kind=kLoop, calls=%fused_computation.130 | loop fusion | flops 20963328 | bytes 5013504 | tf_op jit(solution)/shard_map/reduce_sum | solution.py:107
  234.0 6.2 %fusion.75 = f32[32,8,32]{2,1,0:T(8,128)S(1)} fusion(f32[64,32,8]{0,2,1:T(8,128)S(1)} %bitcast.381, f32[64,32,8]{0,2,1:T(8,128)S(1)} %bitcast.377, f32[64,8,32]{0,2,1:T(8,128)S(1)} %get-tuple-element.29, f32[64,8,32]{0,2,1:T(8,128)S(1)} %get-tuple-element.30, f32[64,8,32]{0,2,1:T(8,128)S(1)} %get-tuple-element.31, f32[64,8,32]{0,2,1:T(8,128)S(1)} %get-tuple-element.32, ...), kind=kLoop, calls=%fused_computation.133 | loop fusion | flops 20963328 | bytes 5013504 | tf_op jit(solution)/shard_map/reduce_sum | solution.py:107
  240.2 6.2 %fusion.59 = f32[32,8,32]{2,1,0:T(8,128)S(1)} fusion(f32[64,32,8]{0,2,1:T(8,128)S(1)} %bitcast.382, f32[64,32,8]{0,2,1:T(8,128)S(1)} %bitcast.378, f32[64,8,32]{0,2,1:T(8,128)S(1)} %get-tuple-element.29, f32[64,8,32]{0,2,1:T(8,128)S(1)} %get-tuple-element.30, f32[64,8,32]{0,2,1:T(8,128)S(1)} %get-tuple-element.31, f32[64,8,32]{0,2,1:T(8,128)S(1)} %get-tuple-element.32, ...), kind=kLoop, calls=%fused_computation.117 | loop fusion | flops 20963328 | bytes 5013504 | tf_op jit(solution)/shard_map/reduce_sum | solution.py:107
  246.5 9.9 %fusion.30 = f32[64,8,32]{0,2,1:T(8,128)S(1)} fusion(f32[32,8,32]{2,1,0:T(8,128)S(1)} %bitcast.314, f32[32,8,32]{2,1,0:T(8,128)S(1)} %bitcast.322, f32[32,8,32]{2,1,0:T(8,128)S(1)} %bitcast.330, f32[32,8,32]{2,1,0:T(8,128)S(1)} %bitcast.338, f32[32,8,32]{2,1,0:T(8,128)S(1)} %bitcast.346, f32[64,32,8]{0,2,1:T(8,128)S(1)} %bitcast.369, ...), kind=kLoop, calls=%fused_computation.88 | loop fusion | flops 22003712 | bytes 4784128 | tf_op jit(solution)/shard_map/reduce_sum | solution.py:105
  256.4 9.9 %fusion.21 = f32[64,8,32]{0,2,1:T(8,128)S(1)} fusion(f32[32,8,32]{2,1,0:T(8,128)S(1)} %bitcast.315, f32[32,8,32]{2,1,0:T(8,128)S(1)} %bitcast.323, f32[32,8,32]{2,1,0:T(8,128)S(1)} %bitcast.331, f32[32,8,32]{2,1,0:T(8,128)S(1)} %bitcast.339, f32[32,8,32]{2,1,0:T(8,128)S(1)} %bitcast.347, f32[64,32,8]{0,2,1:T(8,128)S(1)} %bitcast.370, ...), kind=kLoop, calls=%fused_computation.79 | loop fusion | flops 22003712 | bytes 4784128 | tf_op jit(solution)/shard_map/reduce_sum | solution.py:105
  266.4 1.6 stack.71
  268.0 1.0 reshape_reshape.7
  269.0 3.8 %all-to-all-start.2 = ((f32[8,4,8,256]{3,2,1,0:T(8,128)}), f32[8,4,8,256]{3,2,1,0:T(8,128)S(1)}, u32[]{:S(2)}, u32[]{:S(2)}) async-start(f32[8,4,8,256]{3,2,1,0:T(8,128)} %reshape_reshape.7), calls=%async_computation.2 | async-start | bytes 524288 | tf_op jit(solution)/shard_map/all_to_all | solution.py:29
  273.0 1.8 copy.50
  274.9 1.4 reshape_reshape.6
  276.2 2.8 all-to-all-done.2
  279.0 9.1 %all-to-all-start.1 = ((f32[16,4,8,256]{3,2,1,0:T(8,128)}), f32[16,4,8,256]{3,2,1,0:T(8,128)S(1)}, u32[]{:S(2)}, u32[]{:S(2)}) async-start(f32[16,4,8,256]{3,2,1,0:T(8,128)} %reshape_reshape.6), calls=%async_computation.1 | async-start | bytes 1048576 | tf_op jit(solution)/shard_map/all_to_all | solution.py:29
  288.1 0.6 gather_fusion.3
  288.8 0.7 fusion.84
  289.5 9.7 %all-to-all-done.1 = f32[16,4,8,256]{3,2,1,0:T(8,128)S(1)} async-done(((f32[16,4,8,256]{3,2,1,0:T(8,128)}), f32[16,4,8,256]{3,2,1,0:T(8,128)S(1)}, u32[]{:S(2)}, u32[]{:S(2)}) %all-to-all-start.1) | async-done | bytes 524320 | tf_op jit(solution)/shard_map/all_to_all | solution.py:29
  299.3 0.7 fusion.83
  300.2 3.5 %copy.52 = f32[128,1,4096]{2,1,0:T(1,128)} copy(f32[128,1,4096]{2,0,1:T(8,128)S(1)} %maximum_bitcast_fusion) | data formatting | bytes 4194304 | tf_op jit(solution)/shard_map/all_to_all | solution.py:41
  303.7 4.7 %all-to-all-start.3 = ((f32[128,1,4096]{2,1,0:T(1,128)}), f32[128,1,4096]{2,1,0:T(1,128)S(1)}, u32[]{:S(2)}, u32[]{:S(2)}) async-start(f32[128,1,4096]{2,1,0:T(1,128)} %copy.52), calls=%async_computation.3 | async-start | bytes 4194304 | tf_op jit(solution)/shard_map/all_to_all | solution.py:41
  308.5 2.4 scatter_custom_fusion
  310.9 0.6 gather_fusion.2
  311.6 27.1 %all-to-all-done.3 = f32[128,1,4096]{2,1,0:T(1,128)S(1)} async-done(((f32[128,1,4096]{2,1,0:T(1,128)}), f32[128,1,4096]{2,1,0:T(1,128)S(1)}, u32[]{:S(2)}, u32[]{:S(2)}) %all-to-all-start.3) | async-done | bytes 2097184 | tf_op jit(solution)/shard_map/all_to_all | solution.py:41
  338.7 1.6 copy.66
  340.3 0.5 fusion.81
  340.8 0.5 convolution_add_fusion
  341.2 0.6 copy.67
  (52 shorter events, 1.0 us)
Async XLA Ops:
  6.5 109.0 %all-gather.2.cloned.1.call-start = ((), (), s32[]{:S(2)}) async-start(), calls=%async_computation.4 | async-start | bytes 4718592 | tf_op jit(solution)/shard_map/all_gather | solution.py:147
  28.5 17.6 %copy-start.1 = (s32[512]{0:T(512)S(1)}, s32[512]{0:T(512)}, u32[]{:S(2)}) copy-start(s32[512]{0:T(512)} %param.11) | copy-start | bytes 6148
  28.5 18.4 %copy-start.2 = (bf16[64,32,8,1,8]{0,4,3,2,1:T(8,128)(2,1)S(1)}, bf16[64,32,8,1,8]{0,4,3,2,1:T(8,128)(2,1)}, u32[]{:S(2)}) copy-start(bf16[64,32,8,1,8]{0,4,3,2,1:T(8,128)(2,1)} %param.9) | copy-start | bytes 786436
  118.9 17.0 %copy-start = (bf16[64,32,8,1,256]{0,4,2,1,3:T(8,128)(2,1)S(1)}, bf16[64,32,8,1,256]{0,4,2,1,3:T(8,128)(2,1)}, u32[]{:S(2)}) copy-start(bf16[64,32,8,1,256]{0,4,2,1,3:T(8,128)(2,1)} %copy.42) | copy-start | bytes 25165828
  155.3 35.6 %slice-start = ((s8[16777216]{0:T(1024)(128)(4,1)}), s8[4194304]{0:T(1024)(128)(4,1)S(1)}, s32[]{:S(2)}) async-start(s8[16777216]{0:T(1024)(128)(4,1)} %bitcast.257), calls=%async_computation.5 | async-start | bytes 8388608
  155.3 35.6 %slice-start.1 = ((s8[16777216]{0:T(1024)(128)(4,1)}), s8[4194304]{0:T(1024)(128)(4,1)S(1)}, s32[]{:S(2)}) async-start(s8[16777216]{0:T(1024)(128)(4,1)} %bitcast.257), calls=%async_computation.6 | async-start | bytes 8388608
  167.2 23.7 %slice-start.2 = ((s8[16777216]{0:T(1024)(128)(4,1)}), s8[4194304]{0:T(1024)(128)(4,1)S(1)}, s32[]{:S(2)}) async-start(s8[16777216]{0:T(1024)(128)(4,1)} %bitcast.257), calls=%async_computation.7 | async-start | bytes 8388608
  179.0 11.9 %slice-start.3 = ((s8[16777216]{0:T(1024)(128)(4,1)}), s8[4194304]{0:T(1024)(128)(4,1)S(1)}, s32[]{:S(2)}) async-start(s8[16777216]{0:T(1024)(128)(4,1)} %bitcast.257), calls=%async_computation.8 | async-start | bytes 8388608
  256.4 10.0 %copy-start.3 = (f32[32,8,32]{2,1,0:T(8,128)S(1)}, f32[32,8,32]{2,1,0:T(8,128)}, u32[]{:S(2)}) copy-start(f32[32,8,32]{2,1,0:T(8,128)} %fusion.66) | copy-start | bytes 98308
  256.4 10.0 %copy-start.4 = (f32[32,8,32]{2,1,0:T(8,128)S(1)}, f32[32,8,32]{2,1,0:T(8,128)}, u32[]{:S(2)}) copy-start(f32[32,8,32]{2,1,0:T(8,128)} %fusion.53) | copy-start | bytes 98308
  256.4 10.0 %copy-start.5 = (f32[32,8,32]{2,1,0:T(8,128)S(1)}, f32[32,8,32]{2,1,0:T(8,128)}, u32[]{:S(2)}) copy-start(f32[32,8,32]{2,1,0:T(8,128)} %fusion.50) | copy-start | bytes 98308
  266.4 6.5 %copy-start.6 = (f32[64,8,32]{0,2,1:T(8,128)S(1)}, f32[64,8,32]{0,2,1:T(8,128)}, u32[]{:S(2)}) copy-start(f32[64,8,32]{0,2,1:T(8,128)} %fusion.33) | copy-start | bytes 196612
  269.0 10.0 %all-to-all-start.2 = ((f32[8,4,8,256]{3,2,1,0:T(8,128)}), f32[8,4,8,256]{3,2,1,0:T(8,128)S(1)}, u32[]{:S(2)}, u32[]{:S(2)}) async-start(f32[8,4,8,256]{3,2,1,0:T(8,128)} %reshape_reshape.7), calls=%async_computation.2 | async-start | bytes 524288 | tf_op jit(solution)/shard_map/all_to_all | solution.py:29
  279.0 20.2 %all-to-all-start.1 = ((f32[16,4,8,256]{3,2,1,0:T(8,128)}), f32[16,4,8,256]{3,2,1,0:T(8,128)S(1)}, u32[]{:S(2)}, u32[]{:S(2)}) async-start(f32[16,4,8,256]{3,2,1,0:T(8,128)} %reshape_reshape.6), calls=%async_computation.1 | async-start | bytes 1048576 | tf_op jit(solution)/shard_map/all_to_all | solution.py:29
  303.7 34.9 %all-to-all-start.3 = ((f32[128,1,4096]{2,1,0:T(1,128)}), f32[128,1,4096]{2,1,0:T(1,128)S(1)}, u32[]{:S(2)}, u32[]{:S(2)}) async-start(f32[128,1,4096]{2,1,0:T(1,128)} %copy.52), calls=%async_computation.3 | async-start | bytes 4194304 | tf_op jit(solution)/shard_map/all_to_all | solution.py:41
Sparse Core Ops, SparseCore 0:
  27.8 87.6 all-gather.1
where the time goes:
time: 350 us; the launch traced here: 349 us
  other arithmetic  145 us (41%)
  waiting for transfers between devices  107 us (31%)
  local copies, waits for them, and re-layouts  43.1 us (12%)
  blocking collectives  20.3 us (6%)
  starting transfers between devices  17.6 us (5%)
  between operations  13.9 us (4%)
    reduce_sum x8, other arithmetic, block_gradients(): jnp.sum(part, axis=(1, 3))  86.1 us
    all_gather x1, waiting for transfers between devices, shards(): every_gain = lax.all_gather(col_piece, 'row', axis=0, tiled=True)  67.3 us
    reduce_sum x8, other arithmetic, block_gradients(): jnp.sum(part, axis=(0, 3))  55.6 us
    all_to_all x1, waiting for transfers between devices, side_by_side(): lax.all_to_all(both, axis, split_axis=split_dim, concat_axis=concat_dim,...  27.1 us
    all_to_all x1, blocking collectives, copy_for_each(): return lax.all_to_all(copies, axis, split_axis=0, concat_axis=0, tiled=True)  20.3 us
    unnamed x34, local copies, waits for them, and re-layouts  19.9 us
    all_to_all x2, starting transfers between devices, summed_on_arrival(): lax.all_to_all(blocks, axis, split_axis=0, concat_axis=0, tiled=True)  12.9 us
    all_to_all x2, waiting for transfers between devices, summed_on_arrival(): lax.all_to_all(blocks, axis, split_axis=0, concat_axis=0, tiled=True)  12.5 us
  transfers between devices with their start and end apart: 4, of which 4 were waited for; matrix products, arithmetic and copies ran while one was open for 8% of the time, Pallas kernels for 0%

commit v1 on v0

v1 whole, which is shorter than its diff:
```python
import functools

import jax
import jax.numpy as jnp
from jax import lax
from jax.experimental import pallas as pl
from jax.experimental.pallas import tpu as pltpu
from jax.sharding import PartitionSpec as P

LANES = 128
PER_STEP = 4


def exchanged(x, axis):
    return lax.all_to_all(x, axis, split_axis=0, concat_axis=0, tiled=True)


def swapped(x, group, even):
    return jnp.where(even, pltpu.roll(x, LANES - group, 1), pltpu.roll(x, group, 1))


def summed_groups(x, group):
    half = x + pltpu.roll(x, 2 * group, 1)
    return half + pltpu.roll(half, group, 1)


def replicas(x, group, place):
    kept = jnp.where(place, x, 0.0)
    return summed_groups(kept, group)


def gradients_kernel(
    row_gains, col_gains, residual, coherency, row_side, col_side, col_parts, col_sums, *, group
):
    step = pl.program_id(0)
    per_step, col_count, channels, _ = coherency.shape
    lane = lax.broadcasted_iota(jnp.int32, (channels, LANES), 1)
    index = lane // group
    even = index % 2 == 0
    sign = jnp.where(even, -1.0, 1.0).astype(jnp.float32)

    @pl.when(step == 0)
    def _():
        col_sums[...] = jnp.zeros(col_sums.shape, col_sums.dtype)

        def prepare(k, carry):
            for b in (0, 1):
                own = col_gains[k, :, b * LANES : (b + 1) * LANES]
                col_parts[k, b] = own
                col_parts[k, 2 + b] = sign * swapped(own, group, even)
            return carry

        lax.fori_loop(0, col_count, prepare, 0)

    def one_row(i, carry):
        gains = [row_gains[i, :, b * LANES : (b + 1) * LANES] for b in (0, 1)]
        real = [[replicas(gains[b], group, index == 2 * s) for s in (0, 1)] for b in (0, 1)]
        imag = [[sign * replicas(gains[b], group, index == 2 * s + 1) for s in (0, 1)] for b in (0, 1)]
        weights = residual[i].astype(jnp.float32)
        zero = jnp.zeros((channels, LANES), jnp.float32)
        re_sum = [[zero, zero], [zero, zero]]
        im_sum = [[zero, zero], [zero, zero]]
        for k in range(col_count):
            model = coherency[i, k].astype(jnp.float32)
            m = [model[:, :LANES], model[:, LANES:]]
            sm = [swapped(m[0], group, even), swapped(m[1], group, even)]
            at = k * 8
            g = [
                jnp.broadcast_to(weights[:, at + n : at + n + 1], (channels, LANES))
                for n in range(8)
            ]
            for a in (0, 1):
                product = (
                    g[4 * a] * col_parts[k, 0]
                    + g[4 * a + 1] * col_parts[k, 2]
                    + g[4 * a + 2] * col_parts[k, 1]
                    + g[4 * a + 3] * col_parts[k, 3]
                )
                for c in (0, 1):
                    re_sum[a][c] = re_sum[a][c] + product * m[c]
                    im_sum[a][c] = im_sum[a][c] + product * sm[c]
            t = [
                real[b][0] * m[0] + imag[b][0] * sm[0] + real[b][1] * m[1] + imag[b][1] * sm[1]
                for b in (0, 1)
            ]
            for a in (0, 1):
                col_sums[k, a] += g[2 * a] * t[0] + g[4 + 2 * a] * t[1]
                col_sums[k, 2 + a] += g[2 * a + 1] * t[0] + g[4 + 2 * a + 1] * t[1]
        for a in (0, 1):
            parts = []
            for c in (0, 1):
                parts.append(summed_groups(re_sum[a][c], group))
                parts.append(summed_groups(sign * im_sum[a][c], group))
            joined = parts[3]
            for n in (0, 1, 2):
                joined = jnp.where(index == n, parts[n], joined)
            row_side[i, :, a * LANES : (a + 1) * LANES] = joined
        return carry

    lax.fori_loop(0, per_step, one_row, 0)

    @pl.when(step == pl.num_programs(0) - 1)
    def _():
        def finish(k, carry):
            for a in (0, 1):
                turned = sign * swapped(col_sums[k, 2 + a], group, even)
                col_side[k, :, a * LANES : (a + 1) * LANES] = col_sums[k, a] - turned
            return carry

        lax.fori_loop(0, col_count, finish, 0)


def block_gradients(coherency, residual, row_gains, col_gains, interpret=False):
    rows, cols, channels, width = coherency.shape
    return pl.pallas_call(
        functools.partial(gradients_kernel, group=width // 8),
        grid=(rows // PER_STEP,),
        in_specs=[
            pl.BlockSpec((PER_STEP, channels, width), lambda s: (s, 0, 0)),
            pl.BlockSpec((cols, channels, width), lambda s: (0, 0, 0)),
            pl.BlockSpec((PER_STEP, channels, cols * 8), lambda s: (s, 0, 0)),
            pl.BlockSpec((PER_STEP, cols, channels, width), lambda s: (s, 0, 0, 0)),
        ],
        out_specs=[
            pl.BlockSpec((PER_STEP, channels, width), lambda s: (s, 0, 0)),
            pl.BlockSpec((cols, channels, width), lambda s: (0, 0, 0)),
        ],
        out_shape=[
            jax.ShapeDtypeStruct((rows, channels, width), jnp.float32),
            jax.ShapeDtypeStruct((cols, channels, width), jnp.float32),
        ],
        scratch_shapes=[
            pltpu.VMEM((cols, 4, channels, LANES), jnp.float32),
            pltpu.VMEM((cols, 4, channels, LANES), jnp.float32),
        ],
        compiler_params=pltpu.CompilerParams(dimension_semantics=("arbitrary",)),
        interpret=interpret,
        name="gradients",
    )(row_gains, col_gains, residual, coherency)


def weighted(cotangent, flags):
    rows, cols, channels = cotangent.shape[:3]
    kept = cotangent[:, :, :, 0, :] * flags.astype(cotangent.dtype)[:, :, :, None]
    return jnp.transpose(kept, (0, 2, 1, 3)).reshape(rows, channels, cols * 8)


def one_hot_product(table, values, dims):
    return lax.dot_general(
        table,
        values,
        (dims, ((), ())),
        precision=lax.Precision.HIGHEST,
        preferred_element_type=jnp.float32,
    )


def shards(gains, coherency, cotangent, flags, station_slot):
    stations = station_slot.shape[0]
    share, channels, width = gains.shape
    row_total = lax.axis_size("row")
    col_total = lax.axis_size("col")
    groups = row_total * col_total
    rows, cols = coherency.shape[:2]
    col_start = lax.axis_index("col") * cols

    by_channel = jnp.transpose(gains, (1, 0, 2))
    outward = jnp.broadcast_to(
        by_channel[:, None], (row_total, col_total, share, width)
    ).reshape(groups, share, width)
    channel_gains = exchanged(outward, ("row", "col")).reshape(stations, width)

    identity = jnp.arange(stations, dtype=jnp.int32)[None, :]
    table = (station_slot[:, None] == identity).astype(jnp.float32)
    slot_gains = one_hot_product(table, channel_gains, ((1,), (0,)))
    of_rows = slot_gains.reshape(row_total, rows, width)
    of_col = lax.dynamic_slice_in_dim(slot_gains, col_start, cols)
    of_cols = jnp.broadcast_to(of_col[None], (row_total, cols, width))
    needed = exchanged(jnp.concatenate([of_rows, of_cols], axis=1), "row")
    by_slot = jnp.transpose(needed, (1, 0, 2))

    row_side, col_side = block_gradients(
        coherency[:, :, :, 0, :], weighted(cotangent, flags), by_slot[:rows], by_slot[rows:]
    )

    both = jnp.transpose(jnp.concatenate([row_side, col_side], axis=0), (1, 0, 2))
    arrived = exchanged(both, "row")
    of_slots = arrived[:, :rows].reshape(stations, width)
    col_sum = jnp.sum(arrived[:, rows:], axis=0)
    mine = lax.dynamic_slice_in_dim(of_slots, col_start, cols)
    of_slots = lax.dynamic_update_slice_in_dim(of_slots, mine + col_sum, col_start, 0)
    of_stations = one_hot_product(table, of_slots, ((0,), (0,)))
    homeward = exchanged(of_stations.reshape(groups, share, width), ("row", "col"))
    total = jnp.sum(homeward.reshape(row_total, col_total, share, width), axis=1)
    return jnp.transpose(total, (1, 0, 2))


def solution(mesh):
    placed = (
        P(("row", "col"), None, None),
        P("row", "col", None, None, None),
        P("row", "col", None, None, None),
        P("row", "col", None),
        P(),
    )
    return jax.shard_map(
        shards, mesh=mesh, in_specs=placed, out_specs=P(("row", "col"), None, None), check_vma=False
    )
```

time: 350 us -> 133 us (0.38)
  other arithmetic: 145 us -> 4.09 us
  waiting for transfers between devices: 107 us -> 22.3 us
  Pallas kernels: 0 us -> 48.1 us
  local copies, waits for them, and re-layouts: 43.1 us -> 5.9 us
  blocking collectives: 20.3 us -> 34.6 us
  between operations: 13.9 us -> 0.13 us
    reduce_sum x18 -> x2, other arithmetic: 142 us -> 0.08 us  [the longest x1 0.06 us: shards(): jnp.sum(homeward.reshape(row_total, col_total, share, width), axis=1)]
    all_gather x1 -> x0, waiting for transfers between devices: 67.3 us -> none  [shards(): every_gain = lax.all_gather(col_piece, 'row', axis=0, tiled=True)]
    pallas_call x0 -> x1, Pallas kernels: none -> 48.1 us  [block_gradients(): pl.pallas_call(functools.partial(gradients_kernel, group=width // 8), gri...]
    unnamed x34 -> x3, local copies, waits for them, and re-layouts: 19.9 us -> 0.01 us
    all_to_all x3 -> x2, waiting for transfers between devices: 39.6 us -> 22.3 us  [exchanged(): return lax.all_to_all(x, axis, split_axis=0, concat_axis=0, tiled=True)]
    all_to_all x1 -> x2, blocking collectives: 20.3 us -> 34.6 us  [exchanged(): return lax.all_to_all(x, axis, split_axis=0, concat_axis=0, tiled=True)]
    gather x7 -> x0, local copies, waits for them, and re-layouts: 9.75 us -> none  [the longest x2 4.65 us: shards(): col_gains = jnp.take(every_gain, col_ids, axis=0)]
    another operation x5 -> x0, local copies, waits for them, and re-layouts: 5.86 us -> none  [the longest x2 2.4 us: split_up(): return jnp.moveaxis(x.reshape(*before, length, -1, *after), dim, 0)]
  transfers between devices with their start and end apart: 4 -> 2, of which waited for: 4 -> 2; matrix products, arithmetic and copies ran while one was open for 8% -> 2% of each run, Pallas kernels for 0% -> 0%
where the time goes in v1:
time: 133 us
  Pallas kernels  48.1 us (36%)
  blocking collectives  34.6 us (26%)
  waiting for transfers between devices  22.3 us (17%)
  starting transfers between devices  15 us (11%)
  local copies, waits for them, and re-layouts  5.9 us (4%)
  other arithmetic  4.09 us (3%)
  matrix products  2.48 us (2%)
    pallas_call x1, Pallas kernels, block_gradients(): pl.pallas_call(functools.partial(gradients_kernel, group=width // 8), gri...  48.1 us
    all_to_all x2, blocking collectives, exchanged(): return lax.all_to_all(x, axis, split_axis=0, concat_axis=0, tiled=True)  34.6 us
    all_to_all x2, waiting for transfers between devices, exchanged(): return lax.all_to_all(x, axis, split_axis=0, concat_axis=0, tiled=True)  22.3 us
    all_to_all x2, starting transfers between devices, exchanged(): return lax.all_to_all(x, axis, split_axis=0, concat_axis=0, tiled=True)  15 us
  transfers between devices with their start and end apart: 2, of which 2 were waited for; matrix products, arithmetic and copies ran while one was open for 2% of the time, Pallas kernels for 0%

profile of v1, /device:TPU:1, one launch (start us, length us, event | category | flops | bytes accessed | tf_op | source)
XLA Modules:
  0.0 132.6 jit_solution(14115218835152290839)
XLA Ops:
  0.0 0.8 copy.13
  0.8 0.9 broadcast_in_dim.4
  1.6 11.5 %all-to-all-start = ((f32[128,4,256]{2,1,0:T(4,128)}), f32[128,4,256]{2,1,0:T(4,128)S(1)}, u32[]{:S(2)}, u32[]{:S(2)}) async-start(f32[128,4,256]{2,1,0:T(4,128)} %bitcast.1), calls=%async_computation | async-start | bytes 1048576 | tf_op jit(solution)/shard_map/all_to_all | solution.py:15
  13.1 13.6 %all-to-all-done = f32[128,4,256]{2,1,0:T(4,128)S(1)} async-done(((f32[128,4,256]{2,1,0:T(4,128)}), f32[128,4,256]{2,1,0:T(4,128)S(1)}, u32[]{:S(2)}, u32[]{:S(2)}) %all-to-all-start) | async-done | bytes 524320 | tf_op jit(solution)/shard_map/all_to_all | solution.py:15
  26.7 0.2 reshape.26
  26.9 1.4 %fusion.1 = f32[512,256]{1,0:T(8,128)S(1)} fusion(f32[512,256]{1,0:T(8,128)S(1)} %reshape.26, s32[512]{0:T(512)} %param.9), kind=kOutput, calls=%fused_computation.2 | convolution fusion | flops 805568512 | bytes 1050624 | tf_op jit(solution)/shard_map/dot_general | solution.py:149
  28.3 0.9 pad_maximum_fusion
  29.2 3.5 %all-to-all-start.1 = ((f32[8,96,256]{2,1,0:T(8,128)}), f32[8,96,256]{2,1,0:T(8,128)S(1)}, u32[]{:S(2)}, u32[]{:S(2)}) async-start(f32[8,96,256]{2,1,0:T(8,128)} %pad_maximum_fusion), calls=%async_computation.1 | async-start | bytes 1572864 | tf_op jit(solution)/shard_map/all_to_all | solution.py:15
  32.8 0.7 convert_element_type.4
  33.5 1.2 copy_bitcast_fusion.1
  34.7 1.0 copy.16.residual
  35.7 8.7 %all-to-all-done.1 = f32[8,96,256]{2,1,0:T(8,128)S(1)} async-done(((f32[8,96,256]{2,1,0:T(8,128)}), f32[8,96,256]{2,1,0:T(8,128)S(1)}, u32[]{:S(2)}, u32[]{:S(2)}) %all-to-all-start.1) | async-done | bytes 786464 | tf_op jit(solution)/shard_map/all_to_all | solution.py:15
  44.4 0.5 copy.23
  44.9 0.7 slice.17.col_gains
  45.6 0.0 copy-start
  45.6 0.8 slice.16.row_gains
  46.4 48.1 %gradients.1 = (f32[64,8,256]{2,1,0:T(8,128)}, f32[32,8,256]{2,1,0:T(8,128)}) custom-call(f32[64,8,256]{2,1,0:T(8,128)} %slice.16.row_gains, f32[32,8,256]{2,1,0:T(8,128)} %slice.17.col_gains, bf16[64,8,256]{2,1,0:T(8,128)(2,1)} %copy.16.residual, bf16[64,32,8,256]{3,2,1,0:T(8,128)(2,1)} %bitcast.28), custom_call_target="tpu_custom_call" | custom-call | tf_op jit(solution)/shard_map/gradients/pallas_call | solution.py:115
  94.6 1.2 maximum_bitcast_fusion
  95.7 0.3 copy.17
  96.0 15.5 %all_to_all.20 = f32[8,96,256]{2,1,0:T(8,128)S(1)} all-to-all(f32[8,96,256]{2,1,0:T(8,128)S(1)} %copy.17), channel_id=1, replica_groups=mesh['row'=8,'col'=16] {'row'}, dimensions={0} | all-to-all | bytes 1572864 | tf_op jit(solution)/shard_map/all_to_all | solution.py:15
  111.6 0.0 copy-done
  111.6 1.1 fusion
  112.7 0.1 reshape.30
  112.9 19.0 %all_to_all.21 = f32[128,4,256]{2,1,0:T(4,128)S(1)} all-to-all(f32[128,4,256]{2,1,0:T(4,128)S(1)} %reshape.30), channel_id=1, replica_groups=mesh['row'=8,'col'=16] {'row','col'}, dimensions={0} | all-to-all | bytes 1048576 | tf_op jit(solution)/shard_map/all_to_all | solution.py:15
  131.9 0.1 bitcast_reduce_fusion
  132.0 0.6 copy.18
  (6 shorter events, 0.1 us)
Async XLA Ops:
  1.6 25.1 %all-to-all-start = ((f32[128,4,256]{2,1,0:T(4,128)}), f32[128,4,256]{2,1,0:T(4,128)S(1)}, u32[]{:S(2)}, u32[]{:S(2)}) async-start(f32[128,4,256]{2,1,0:T(4,128)} %bitcast.1), calls=%async_computation | async-start | bytes 1048576 | tf_op jit(solution)/shard_map/all_to_all | solution.py:15
  29.2 15.2 %all-to-all-start.1 = ((f32[8,96,256]{2,1,0:T(8,128)}), f32[8,96,256]{2,1,0:T(8,128)S(1)}, u32[]{:S(2)}, u32[]{:S(2)}) async-start(f32[8,96,256]{2,1,0:T(8,128)} %pad_maximum_fusion), calls=%async_computation.1 | async-start | bytes 1572864 | tf_op jit(solution)/shard_map/all_to_all | solution.py:15
  45.6 66.0 %copy-start = (s32[512]{0:T(512)S(1)}, s32[512]{0:T(512)}, u32[]{:S(2)}) copy-start(s32[512]{0:T(512)} %param.9) | copy-start | bytes 6148

commit v2 on v1

--- a/solution.py
+++ b/solution.py
@@ -9,6 +9,7 @@
 
 LANES = 128
 PER_STEP = 4
+UNROLL = 16
 
 
 def exchanged(x, axis):
@@ -30,7 +31,18 @@
 
 
 def gradients_kernel(
-    row_gains, col_gains, residual, coherency, row_side, col_side, col_parts, col_sums, *, group
+    row_gains,
+    col_gains,
+    residual,
+    coherency,
+    spread,
+    swap,
+    row_side,
+    col_side,
+    col_parts,
+    col_sums,
+    *,
+    group,
 ):
     step = pl.program_id(0)
     per_step, col_count, channels, _ = coherency.shape
@@ -56,41 +68,50 @@
         gains = [row_gains[i, :, b * LANES : (b + 1) * LANES] for b in (0, 1)]
         real = [[replicas(gains[b], group, index == 2 * s) for s in (0, 1)] for b in (0, 1)]
         imag = [[sign * replicas(gains[b], group, index == 2 * s + 1) for s in (0, 1)] for b in (0, 1)]
-        weights = residual[i].astype(jnp.float32)
         zero = jnp.zeros((channels, LANES), jnp.float32)
-        re_sum = [[zero, zero], [zero, zero]]
-        im_sum = [[zero, zero], [zero, zero]]
-        for k in range(col_count):
-            model = coherency[i, k].astype(jnp.float32)
-            m = [model[:, :LANES], model[:, LANES:]]
-            sm = [swapped(m[0], group, even), swapped(m[1], group, even)]
-            at = k * 8
-            g = [
-                jnp.broadcast_to(weights[:, at + n : at + n + 1], (channels, LANES))
-                for n in range(8)
-            ]
-            for a in (0, 1):
-                product = (
-                    g[4 * a] * col_parts[k, 0]
-                    + g[4 * a + 1] * col_parts[k, 2]
-                    + g[4 * a + 2] * col_parts[k, 1]
-                    + g[4 * a + 3] * col_parts[k, 3]
-                )
-                for c in (0, 1):
-                    re_sum[a][c] = re_sum[a][c] + product * m[c]
-                    im_sum[a][c] = im_sum[a][c] + product * sm[c]
-            t = [
-                real[b][0] * m[0] + imag[b][0] * sm[0] + real[b][1] * m[1] + imag[b][1] * sm[1]
-                for b in (0, 1)
-            ]
-            for a in (0, 1):
-                col_sums[k, a] += g[2 * a] * t[0] + g[4 + 2 * a] * t[1]
-                col_sums[k, 2 + a] += g[2 * a + 1] * t[0] + g[4 + 2 * a + 1] * t[1]
+
+        def some_cols(block, sums):
+            sums = list(sums)
+            weights = jnp.dot(
+                residual[i, block], spread[...], preferred_element_type=jnp.float32
+            )
+            models = coherency[i, pl.ds(block * UNROLL, UNROLL)].reshape(
+                UNROLL * channels, 2 * LANES
+            )
+            turned = jnp.dot(models, swap[...], preferred_element_type=jnp.float32)
+            for j in range(UNROLL):
+                k = block * UNROLL + j
+                at = slice(j * channels, (j + 1) * channels)
+                model = models[at].astype(jnp.float32)
+                m = [model[:, :LANES], model[:, LANES:]]
+                sm = [turned[at, :LANES], turned[at, LANES:]]
+                g = [weights[at, n * LANES : (n + 1) * LANES] for n in range(8)]
+                for a in (0, 1):
+                    product = (
+                        g[4 * a] * col_parts[k, 0]
+                        + g[4 * a + 1] * col_parts[k, 2]
+                        + g[4 * a + 2] * col_parts[k, 1]
+                        + g[4 * a + 3] * col_parts[k, 3]
+                    )
+                    for c in (0, 1):
+                        to = 4 * a + 2 * c
+                        sums[to] = sums[to] + product * m[c]
+                        sums[to + 1] = sums[to + 1] + product * sm[c]
+                t = [
+                    real[b][0] * m[0] + imag[b][0] * sm[0] + real[b][1] * m[1] + imag[b][1] * sm[1]
+                    for b in (0, 1)
+                ]
+                for a in (0, 1):
+                    col_sums[k, a] += g[2 * a] * t[0] + g[4 + 2 * a] * t[1]
+                    col_sums[k, 2 + a] += g[2 * a + 1] * t[0] + g[4 + 2 * a + 1] * t[1]
+            return tuple(sums)
+
+        sums = lax.fori_loop(0, col_count // UNROLL, some_cols, (zero,) * 8)
         for a in (0, 1):
             parts = []
             for c in (0, 1):
-                parts.append(summed_groups(re_sum[a][c], group))
-                parts.append(summed_groups(sign * im_sum[a][c], group))
+                parts.append(summed_groups(sums[4 * a + 2 * c], group))
+                parts.append(summed_groups(sign * sums[4 * a + 2 * c + 1], group))
             joined = parts[3]
             for n in (0, 1, 2):
                 joined = jnp.where(index == n, parts[n], joined)
@@ -112,14 +133,22 @@
 
 def block_gradients(coherency, residual, row_gains, col_gains, interpret=False):
     rows, cols, channels, width = coherency.shape
+    group = width // 8
+    lane = jnp.arange(8 * LANES, dtype=jnp.int32)
+    spread = (lane[None, :8] == (lane[:, None] // LANES)).T.astype(jnp.bfloat16)
+    part = lane[:width]
+    partner = part + jnp.where(part // group % 2 == 0, group, -group)
+    swap = (part[:, None] == partner[None, :]).astype(jnp.bfloat16)
     return pl.pallas_call(
         functools.partial(gradients_kernel, group=width // 8),
         grid=(rows // PER_STEP,),
         in_specs=[
             pl.BlockSpec((PER_STEP, channels, width), lambda s: (s, 0, 0)),
             pl.BlockSpec((cols, channels, width), lambda s: (0, 0, 0)),
-            pl.BlockSpec((PER_STEP, channels, cols * 8), lambda s: (s, 0, 0)),
+            pl.BlockSpec((PER_STEP, cols // UNROLL, UNROLL * channels, 8), lambda s: (s, 0, 0, 0)),
             pl.BlockSpec((PER_STEP, cols, channels, width), lambda s: (s, 0, 0, 0)),
+            pl.BlockSpec((8, 8 * LANES), lambda s: (0, 0)),
+            pl.BlockSpec((width, width), lambda s: (0, 0)),
         ],
         out_specs=[
             pl.BlockSpec((PER_STEP, channels, width), lambda s: (s, 0, 0)),
@@ -136,13 +165,13 @@
         compiler_params=pltpu.CompilerParams(dimension_semantics=("arbitrary",)),
         interpret=interpret,
         name="gradients",
-    )(row_gains, col_gains, residual, coherency)
+    )(row_gains, col_gains, residual, coherency, spread, swap)
 
 
 def weighted(cotangent, flags):
     rows, cols, channels = cotangent.shape[:3]
     kept = cotangent[:, :, :, 0, :] * flags.astype(cotangent.dtype)[:, :, :, None]
-    return jnp.transpose(kept, (0, 2, 1, 3)).reshape(rows, channels, cols * 8)
+    return kept.reshape(rows, cols // UNROLL, UNROLL * channels, 8)
 
 
 def one_hot_product(table, values, dims):

time: 133 us -> 148 us (1.11)
  Pallas kernels: 48.1 us -> 63 us
  waiting for transfers between devices: 22.3 us -> 9.99 us
  local copies, waits for them, and re-layouts: 5.9 us -> 12.8 us
  other arithmetic: 4.09 us -> 9.53 us
    pallas_call x1, Pallas kernels: 48.1 us -> 63 us  [block_gradients(): pl.pallas_call(functools.partial(gradients_kernel, group=width // 8), gri...]
    all_to_all x2, waiting for transfers between devices: 22.3 us -> 9.99 us  [exchanged(): return lax.all_to_all(x, axis, split_axis=0, concat_axis=0, tiled=True)]
    unnamed x3 -> x6, local copies, waits for them, and re-layouts: 0.01 us -> 7.73 us
    mul x0 -> x1, other arithmetic: none -> 5.81 us  [weighted(): cotangent[:, :, :, 0, :] * flags.astype(cotangent.dtype)[:, :, :, None]]
  transfers between devices with their start and end apart: 2 -> 2, of which waited for: 2 -> 2; matrix products, arithmetic and copies ran while one was open for 2% -> 10% of each run, Pallas kernels for 0% -> 0%
where the time goes in v2:
time: 148 us; the launch traced here: 147 us
  Pallas kernels  63 us (43%)
  blocking collectives  35 us (24%)
  starting transfers between devices  15 us (10%)
  local copies, waits for them, and re-layouts  12.8 us (9%)
  waiting for transfers between devices  9.99 us (7%)
  other arithmetic  9.53 us (6%)
  matrix products  1.8 us (1%)
    pallas_call x1, Pallas kernels, block_gradients(): pl.pallas_call(functools.partial(gradients_kernel, group=width // 8), gri...  63 us
    all_to_all x2, blocking collectives, exchanged(): return lax.all_to_all(x, axis, split_axis=0, concat_axis=0, tiled=True)  35 us
    all_to_all x2, starting transfers between devices, exchanged(): return lax.all_to_all(x, axis, split_axis=0, concat_axis=0, tiled=True)  15 us
    all_to_all x2, waiting for transfers between devices, exchanged(): return lax.all_to_all(x, axis, split_axis=0, concat_axis=0, tiled=True)  9.99 us
    unnamed x6, local copies, waits for them, and re-layouts  7.73 us
    mul x1, other arithmetic, weighted(): cotangent[:, :, :, 0, :] * flags.astype(cotangent.dtype)[:, :, :, None]  5.81 us
  transfers between devices with their start and end apart: 2, of which 2 were waited for; matrix products, arithmetic and copies ran while one was open for 10% of the time, Pallas kernels for 0%

profile of v2, /device:TPU:1, one launch (start us, length us, event | category | flops | bytes accessed | tf_op | source)
XLA Modules:
  0.0 147.3 jit_solution(4345296700309758963)
XLA Ops:
  0.0 0.0 copy-start
  0.0 0.0 copy-start.1
  0.0 0.8 copy.14
  0.8 0.9 broadcast_in_dim.8
  1.7 11.5 %all-to-all-start = ((f32[128,4,256]{2,1,0:T(4,128)}), f32[128,4,256]{2,1,0:T(4,128)S(1)}, u32[]{:S(2)}, u32[]{:S(2)}) async-start(f32[128,4,256]{2,1,0:T(4,128)} %bitcast.1), calls=%async_computation | async-start | bytes 1048576 | tf_op jit(solution)/shard_map/all_to_all | solution.py:16
  13.2 7.7 %copy.16 = bf16[64,32,8,1,8]{4,2,1,0,3:T(8,128)(2,1)} copy(bf16[64,32,8,1,8]{0,4,3,2,1:T(8,128)(2,1)} %param.7) | data formatting | bytes 524288 | tf_op args[2]
  20.9 0.0 copy-done
  20.9 0.1 copy.17
  21.1 0.8 compare_convert_fusion.swap
  21.9 4.9 %all-to-all-done = f32[128,4,256]{2,1,0:T(4,128)S(1)} async-done(((f32[128,4,256]{2,1,0:T(4,128)}), f32[128,4,256]{2,1,0:T(4,128)S(1)}, u32[]{:S(2)}, u32[]{:S(2)}) %all-to-all-start) | async-done | bytes 524320 | tf_op jit(solution)/shard_map/all_to_all | solution.py:16
  26.7 0.2 reshape.66
  26.9 0.0 copy-done.1
  26.9 0.7 fusion.1
  27.7 1.0 pad_maximum_fusion
  28.7 3.5 %all-to-all-start.1 = ((f32[8,96,256]{2,1,0:T(8,128)}), f32[8,96,256]{2,1,0:T(8,128)S(1)}, u32[]{:S(2)}, u32[]{:S(2)}) async-start(f32[8,96,256]{2,1,0:T(8,128)} %pad_maximum_fusion), calls=%async_computation.1 | async-start | bytes 1572864 | tf_op jit(solution)/shard_map/all_to_all | solution.py:16
  32.2 0.7 compare_convert_fusion.1.spread
  32.9 5.8 %broadcast_multiply_fusion.residual = bf16[64,2,128,8]{3,2,1,0:T(8,128)(2,1)} fusion(bf16[64,2,128,8]{3,2,1,0:T(8,128)(2,1)} %bitcast.20, bf16[64,2,128]{2,1,0:T(2,128)(2,1)S(1)} %copy.17), kind=kLoop, calls=%fused_computation | loop fusion | flops 131072 | bytes 557056 | tf_op jit(solution)/shard_map/mul | solution.py:173
  38.7 5.1 %all-to-all-done.1 = f32[8,96,256]{2,1,0:T(8,128)S(1)} async-done(((f32[8,96,256]{2,1,0:T(8,128)}), f32[8,96,256]{2,1,0:T(8,128)S(1)}, u32[]{:S(2)}, u32[]{:S(2)}) %all-to-all-start.1) | async-done | bytes 786464 | tf_op jit(solution)/shard_map/all_to_all | solution.py:16
  43.8 0.5 copy.23
  44.3 0.8 slice.24.row_gains
  45.1 0.7 slice.25.col_gains
  45.8 63.0 %gradients.1 = (f32[64,8,256]{2,1,0:T(8,128)}, f32[32,8,256]{2,1,0:T(8,128)}) custom-call(f32[64,8,256]{2,1,0:T(8,128)} %slice.24.row_gains, f32[32,8,256]{2,1,0:T(8,128)} %slice.25.col_gains, bf16[64,2,128,8]{3,2,1,0:T(8,128)(2,1)} %broadcast_multiply_fusion.residual, bf16[64,32,8,256]{3,2,1,0:T(8,128)(2,1)} %bitcast.21, ...), custom_call_target="tpu_custom_call" | custom-call | tf_op jit(solution)/shard_map/gradients/pallas_call | solution.py:142
  108.8 1.2 maximum_bitcast_fusion
  110.0 0.3 copy.18
  110.2 15.5 %all_to_all.20 = f32[8,96,256]{2,1,0:T(8,128)S(1)} all-to-all(f32[8,96,256]{2,1,0:T(8,128)S(1)} %copy.18), channel_id=1, replica_groups=mesh['row'=8,'col'=16] {'row'}, dimensions={0} | all-to-all | bytes 1572864 | tf_op jit(solution)/shard_map/all_to_all | solution.py:16
  125.8 1.1 fusion
  127.0 0.1 reshape.69
  127.1 19.5 %all_to_all.21 = f32[128,4,256]{2,1,0:T(4,128)S(1)} all-to-all(f32[128,4,256]{2,1,0:T(4,128)S(1)} %reshape.69), channel_id=1, replica_groups=mesh['row'=8,'col'=16] {'row','col'}, dimensions={0} | all-to-all | bytes 1048576 | tf_op jit(solution)/shard_map/all_to_all | solution.py:16
  146.6 0.1 bitcast_reduce_fusion
  146.6 0.6 copy.19
  (13 shorter events, 0.2 us)
Async XLA Ops:
  0.0 20.9 %copy-start = (s32[64,32,1]{0,2,1:T(1,128)S(1)}, s32[64,32,1]{0,2,1:T(1,128)}, u32[]{:S(2)}) copy-start(s32[64,32,1]{0,2,1:T(1,128)} %param.8) | copy-start | bytes 24580
  0.0 26.9 %copy-start.1 = (s32[512]{0:T(512)S(1)}, s32[512]{0:T(512)}, u32[]{:S(2)}) copy-start(s32[512]{0:T(512)} %param.9) | copy-start | bytes 6148
  1.7 25.1 %all-to-all-start = ((f32[128,4,256]{2,1,0:T(4,128)}), f32[128,4,256]{2,1,0:T(4,128)S(1)}, u32[]{:S(2)}, u32[]{:S(2)}) async-start(f32[128,4,256]{2,1,0:T(4,128)} %bitcast.1), calls=%async_computation | async-start | bytes 1048576 | tf_op jit(solution)/shard_map/all_to_all | solution.py:16
  28.7 15.2 %all-to-all-start.1 = ((f32[8,96,256]{2,1,0:T(8,128)}), f32[8,96,256]{2,1,0:T(8,128)S(1)}, u32[]{:S(2)}, u32[]{:S(2)}) async-start(f32[8,96,256]{2,1,0:T(8,128)} %pad_maximum_fusion), calls=%async_computation.1 | async-start | bytes 1572864 | tf_op jit(solution)/shard_map/all_to_all | solution.py:16

commit v3 on v1

v3 whole, which is shorter than its diff:
```python
import functools

import jax
import jax.numpy as jnp
from jax import lax
from jax.experimental import pallas as pl
from jax.experimental.pallas import tpu as pltpu
from jax.sharding import PartitionSpec as P

LANES = 128
PER_STEP = 8
BATCH = 8


def exchanged(x, axis):
    return lax.all_to_all(x, axis, split_axis=0, concat_axis=0, tiled=True)


def swapped(x, group, even):
    return jnp.where(even, pltpu.roll(x, LANES - group, 1), pltpu.roll(x, group, 1))


def summed_groups(x, group):
    half = x + pltpu.roll(x, 2 * group, 1)
    return half + pltpu.roll(half, group, 1)


def replicas(x, group, place):
    kept = jnp.where(place, x, 0.0)
    return summed_groups(kept, group)


def swap_kernel(coherency, swap, turned):
    rows = coherency.shape[0] * coherency.shape[1] * coherency.shape[2]
    flat = coherency[...].reshape(rows, coherency.shape[3])
    product = jnp.dot(flat, swap[...], preferred_element_type=jnp.float32)
    turned[...] = product.astype(turned.dtype).reshape(turned.shape)


def swapped_pairs(coherency, interpret=False):
    rows, cols, channels, width = coherency.shape
    group = width // 8
    part = jnp.arange(width, dtype=jnp.int32)
    partner = part + jnp.where(part // group % 2 == 0, group, -group)
    swap = (part[:, None] == partner[None, :]).astype(coherency.dtype)
    block = pl.BlockSpec((PER_STEP, cols, channels, width), lambda s: (s, 0, 0, 0))
    return pl.pallas_call(
        swap_kernel,
        grid=(rows // PER_STEP,),
        in_specs=[block, pl.BlockSpec((width, width), lambda s: (0, 0))],
        out_specs=block,
        out_shape=jax.ShapeDtypeStruct(coherency.shape, coherency.dtype),
        compiler_params=pltpu.CompilerParams(dimension_semantics=("arbitrary",)),
        cost_estimate=pl.CostEstimate(
            flops=2 * width * coherency.size, bytes_accessed=4 * coherency.size, transcendentals=0
        ),
        interpret=interpret,
        name="swap",
    )(coherency, swap)


def gradients_kernel(
    row_gains,
    col_gains,
    residual,
    coherency,
    turned,
    spread,
    row_side,
    col_side,
    row_parts,
    row_sums,
    col_parts,
    col_sums,
    weights_even,
    weights_odd,
    *,
    group,
):
    step = pl.program_id(0)
    per_step, col_count, channels, _ = coherency.shape
    row_count = row_gains.shape[0]
    lane = lax.broadcasted_iota(jnp.int32, (channels, LANES), 1)
    index = lane // group
    even = index % 2 == 0
    sign = jnp.where(even, -1.0, 1.0).astype(jnp.float32)

    @pl.when(step == 0)
    def _():
        col_sums[...] = jnp.zeros(col_sums.shape, col_sums.dtype)

        def prepare_cols(block, carry):
            for j in range(BATCH):
                k = block * BATCH + j
                for b in (0, 1):
                    own = col_gains[k, :, b * LANES : (b + 1) * LANES]
                    col_parts[k, b] = own
                    col_parts[k, 2 + b] = sign * swapped(own, group, even)
            return carry

        lax.fori_loop(0, col_count // BATCH, prepare_cols, 0)

        def prepare_rows(block, carry):
            for j in range(BATCH):
                i = block * BATCH + j
                for b in (0, 1):
                    own = row_gains[i, :, b * LANES : (b + 1) * LANES]
                    for n in range(4):
                        copies = replicas(own, group, index == n)
                        row_parts[i, 4 * b + n] = copies if n % 2 == 0 else sign * copies
            return carry

        lax.fori_loop(0, row_count // BATCH, prepare_rows, 0)

    def spread_out(i, weights):
        weights[...] = lax.dot_general(
            residual[i], spread[...], (((0,), (0,)), ((), ())), preferred_element_type=jnp.float32
        )

    def one_row(i, weights):
        row = step * per_step + i
        zero = jnp.zeros((channels, LANES), jnp.float32)
        sums = [zero] * 8
        for k in range(col_count):
            at = slice(k * channels, (k + 1) * channels)
            model = coherency[i, k].astype(jnp.float32)
            other = turned[i, k].astype(jnp.float32)
            m = [model[:, :LANES], model[:, LANES:]]
            sm = [other[:, :LANES], other[:, LANES:]]
            g = [weights[at, n * LANES : (n + 1) * LANES] for n in range(8)]
            for a in (0, 1):
                product = (
                    g[4 * a] * col_parts[k, 0]
                    + g[4 * a + 1] * col_parts[k, 2]
                    + g[4 * a + 2] * col_parts[k, 1]
                    + g[4 * a + 3] * col_parts[k, 3]
                )
                for c in (0, 1):
                    to = 4 * a + 2 * c
                    sums[to] = sums[to] + product * m[c]
                    sums[to + 1] = sums[to + 1] + product * sm[c]
            t = [
                row_parts[row, 4 * b] * m[0]
                + row_parts[row, 4 * b + 1] * sm[0]
                + row_parts[row, 4 * b + 2] * m[1]
                + row_parts[row, 4 * b + 3] * sm[1]
                for b in (0, 1)
            ]
            for a in (0, 1):
                col_sums[k, a] += g[2 * a] * t[0] + g[4 + 2 * a] * t[1]
                col_sums[k, 2 + a] += g[2 * a + 1] * t[0] + g[4 + 2 * a + 1] * t[1]
        for n in range(8):
            row_sums[row, n] = sums[n]

    spread_out(0, weights_even)

    def two_rows(half, carry):
        i = 2 * half
        spread_out(i + 1, weights_odd)
        one_row(i, weights_even)
        spread_out(jnp.minimum(i + 2, per_step - 1), weights_even)
        one_row(i + 1, weights_odd)
        return carry

    lax.fori_loop(0, per_step // 2, two_rows, 0)

    @pl.when(step == pl.num_programs(0) - 1)
    def _():
        def finish_rows(block, carry):
            for j in range(BATCH):
                i = block * BATCH + j
                for a in (0, 1):
                    joined = None
                    for n in range(4):
                        own = row_sums[i, 4 * a + n]
                        part = summed_groups(own if n % 2 == 0 else sign * own, group)
                        joined = part if n == 0 else jnp.where(index == n, part, joined)
                    row_side[i, :, a * LANES : (a + 1) * LANES] = joined
            return carry

        lax.fori_loop(0, row_count // BATCH, finish_rows, 0)

        def finish_cols(block, carry):
            for j in range(BATCH):
                k = block * BATCH + j
                for a in (0, 1):
                    back = sign * swapped(col_sums[k, 2 + a], group, even)
                    col_side[k, :, a * LANES : (a + 1) * LANES] = col_sums[k, a] - back
            return carry

        lax.fori_loop(0, col_count // BATCH, finish_cols, 0)


def block_gradients(coherency, turned, residual, row_gains, col_gains, interpret=False):
    rows, cols, channels, width = coherency.shape
    lane = jnp.arange(8 * LANES, dtype=jnp.int32)
    spread = (lane[None, :8] == (lane[:, None] // LANES)).T.astype(jnp.bfloat16)
    block = pl.BlockSpec((PER_STEP, cols, channels, width), lambda s: (s, 0, 0, 0))
    every_row = pl.BlockSpec((rows, channels, width), lambda s: (0, 0, 0))
    every_col = pl.BlockSpec((cols, channels, width), lambda s: (0, 0, 0))
    return pl.pallas_call(
        functools.partial(gradients_kernel, group=width // 8),
        grid=(rows // PER_STEP,),
        in_specs=[
            every_row,
            every_col,
            pl.BlockSpec((PER_STEP, 8, cols * channels), lambda s: (s, 0, 0)),
            block,
            block,
            pl.BlockSpec((8, 8 * LANES), lambda s: (0, 0)),
        ],
        out_specs=[every_row, every_col],
        out_shape=[
            jax.ShapeDtypeStruct((rows, channels, width), jnp.float32),
            jax.ShapeDtypeStruct((cols, channels, width), jnp.float32),
        ],
        scratch_shapes=[
            pltpu.VMEM((rows, 8, channels, LANES), jnp.float32),
            pltpu.VMEM((rows, 8, channels, LANES), jnp.float32),
            pltpu.VMEM((cols, 4, channels, LANES), jnp.float32),
            pltpu.VMEM((cols, 4, channels, LANES), jnp.float32),
            pltpu.VMEM((cols * channels, 8 * LANES), jnp.float32),
            pltpu.VMEM((cols * channels, 8 * LANES), jnp.float32),
        ],
        compiler_params=pltpu.CompilerParams(dimension_semantics=("arbitrary",)),
        interpret=interpret,
        name="gradients",
    )(row_gains, col_gains, residual, coherency, turned, spread)


def weighted(cotangent, flags):
    rows, cols, channels = cotangent.shape[:3]
    kept = cotangent[:, :, :, 0, :] * flags.astype(cotangent.dtype)[:, :, :, None]
    return jnp.transpose(kept, (0, 3, 1, 2)).reshape(rows, 8, cols * channels)


def one_hot_product(table, values, dims):
    return lax.dot_general(
        table,
        values,
        (dims, ((), ())),
        precision=lax.Precision.HIGHEST,
        preferred_element_type=jnp.float32,
    )


def shards(gains, coherency, cotangent, flags, station_slot):
    stations = station_slot.shape[0]
    share, channels, width = gains.shape
    row_total = lax.axis_size("row")
    col_total = lax.axis_size("col")
    groups = row_total * col_total
    rows, cols = coherency.shape[:2]
    col_start = lax.axis_index("col") * cols

    by_channel = jnp.transpose(gains, (1, 0, 2))
    outward = jnp.broadcast_to(
        by_channel[:, None], (row_total, col_total, share, width)
    ).reshape(groups, share, width)
    channel_gains = exchanged(outward, ("row", "col"))
    models = coherency[:, :, :, 0, :]
    channel_gains, turned = lax.optimization_barrier((channel_gains, swapped_pairs(models)))
    channel_gains = channel_gains.reshape(stations, width)

    identity = jnp.arange(stations, dtype=jnp.int32)[None, :]
    table = (station_slot[:, None] == identity).astype(jnp.float32)
    slot_gains = one_hot_product(table, channel_gains, ((1,), (0,)))
    of_rows = slot_gains.reshape(row_total, rows, width)
    of_col = lax.dynamic_slice_in_dim(slot_gains, col_start, cols)
    of_cols = jnp.broadcast_to(of_col[None], (row_total, cols, width))
    needed = exchanged(jnp.concatenate([of_rows, of_cols], axis=1), "row")
    by_slot = jnp.transpose(needed, (1, 0, 2))

    row_side, col_side = block_gradients(
        models,
        turned,
        weighted(cotangent, flags),
        by_slot[:rows],
        by_slot[rows:],
    )

    both = jnp.transpose(jnp.concatenate([row_side, col_side], axis=0), (1, 0, 2))
    arrived = exchanged(both, "row")
    of_slots = arrived[:, :rows].reshape(stations, width)
    col_sum = jnp.sum(arrived[:, rows:], axis=0)
    mine = lax.dynamic_slice_in_dim(of_slots, col_start, cols)
    of_slots = lax.dynamic_update_slice_in_dim(of_slots, mine + col_sum, col_start, 0)
    of_stations = one_hot_product(table, of_slots, ((0,), (0,)))
    homeward = exchanged(of_stations.reshape(groups, share, width), ("row", "col"))
    total = jnp.sum(homeward.reshape(row_total, col_total, share, width), axis=1)
    return jnp.transpose(total, (1, 0, 2))


def solution(mesh):
    placed = (
        P(("row", "col"), None, None),
        P("row", "col", None, None, None),
        P("row", "col", None, None, None),
        P("row", "col", None),
        P(),
    )
    return jax.shard_map(
        shards, mesh=mesh, in_specs=placed, out_specs=P(("row", "col"), None, None), check_vma=False
    )
```

time: 133 us -> 122 us (0.917)
  waiting for transfers between devices: 22.3 us -> 12.1 us
  blocking collectives: 34.6 us -> 37.4 us
  Pallas kernels: 48.1 us -> 45.6 us
    pallas_call x1, Pallas kernels: 48.1 us -> 35.1 us  [block_gradients(): pl.pallas_call(functools.partial(gradients_kernel, group=width // 8), gri...]
    pallas_call x0 -> x1, Pallas kernels: none -> 10.4 us  [swapped_pairs(): pl.pallas_call(swap_kernel, grid=(rows // PER_STEP,), in_specs=[block, pl...]
    all_to_all x2, waiting for transfers between devices: 22.3 us -> 12.1 us  [exchanged(): return lax.all_to_all(x, axis, split_axis=0, concat_axis=0, tiled=True)]
    all_to_all x2, blocking collectives: 34.6 us -> 37.4 us  [exchanged(): return lax.all_to_all(x, axis, split_axis=0, concat_axis=0, tiled=True)]
    convert_element_type x0 -> x2, other arithmetic: none -> 1.35 us  [the longest x1 0.68 us: block_gradients(): spread = (lane[None, :8] == lane[:, None] // LANES).T.astype(jnp.bfloat16)]
  transfers between devices with their start and end apart: 2 -> 2, of which waited for: 2 -> 2; matrix products, arithmetic and copies ran while one was open for 2% -> 2% of each run, Pallas kernels for 0% -> 9%
where the time goes in v3:
time: 122 us
  Pallas kernels  45.6 us (37%)
  blocking collectives  37.4 us (31%)
  starting transfers between devices  15 us (12%)
  waiting for transfers between devices  12.1 us (10%)
  local copies, waits for them, and re-layouts  6.18 us (5%)
  other arithmetic  3.67 us (3%)
  matrix products  1.8 us (1%)
    all_to_all x2, blocking collectives, exchanged(): return lax.all_to_all(x, axis, split_axis=0, concat_axis=0, tiled=True)  37.4 us
    pallas_call x1, Pallas kernels, block_gradients(): pl.pallas_call(functools.partial(gradients_kernel, group=width // 8), gri...  35.1 us
    all_to_all x2, starting transfers between devices, exchanged(): return lax.all_to_all(x, axis, split_axis=0, concat_axis=0, tiled=True)  15 us
    all_to_all x2, waiting for transfers between devices, exchanged(): return lax.all_to_all(x, axis, split_axis=0, concat_axis=0, tiled=True)  12.1 us
    pallas_call x1, Pallas kernels, swapped_pairs(): pl.pallas_call(swap_kernel, grid=(rows // PER_STEP,), in_specs=[block, pl...  10.4 us
  transfers between devices with their start and end apart: 2, of which 2 were waited for; matrix products, arithmetic and copies ran while one was open for 2% of the time, Pallas kernels for 9%

profile of v3, /device:TPU:1, one launch (start us, length us, event | category | flops | bytes accessed | tf_op | source)
XLA Modules:
  0.0 121.9 jit_solution(14487736107660528706)
XLA Ops:
  0.0 0.8 copy.13
  0.8 0.9 broadcast_in_dim.10
  1.7 11.5 %all-to-all-start = ((f32[128,4,256]{2,1,0:T(4,128)}), f32[128,4,256]{2,1,0:T(4,128)S(1)}, u32[]{:S(2)}, u32[]{:S(2)}) async-start(f32[128,4,256]{2,1,0:T(4,128)} %bitcast.1), calls=%async_computation | async-start | bytes 1048576 | tf_op jit(solution)/shard_map/all_to_all | solution.py:16
  13.2 0.7 fusion.4.swap
  13.9 0.0 copy-start.2
  13.9 0.0 copy-start.1
  13.9 0.0 copy-start
  13.9 10.4 %swap.1.turned = bf16[64,32,8,256]{3,2,1,0:T(8,128)(2,1)} custom-call(bf16[64,32,8,256]{3,2,1,0:T(8,128)(2,1)} %bitcast.23, bf16[256,256]{1,0:T(8,128)(2,1)} %fusion.4.swap), custom_call_target="tpu_custom_call" | custom-call | flops 2147483648 | bytes 16777216 | tf_op jit(solution)/shard_map/swap/pallas_call | solution.py:47
  24.3 2.4 %all-to-all-done = f32[128,4,256]{2,1,0:T(4,128)S(1)} async-done(((f32[128,4,256]{2,1,0:T(4,128)}), f32[128,4,256]{2,1,0:T(4,128)S(1)}, u32[]{:S(2)}, u32[]{:S(2)}) %all-to-all-start) | async-done | bytes 524320 | tf_op jit(solution)/shard_map/all_to_all | solution.py:16
  26.8 0.2 reshape.92
  26.9 0.0 copy-done.2
  27.0 0.7 fusion.1
  27.7 1.0 pad_maximum_fusion
  28.7 3.5 %all-to-all-start.1 = ((f32[8,96,256]{2,1,0:T(8,128)}), f32[8,96,256]{2,1,0:T(8,128)S(1)}, u32[]{:S(2)}, u32[]{:S(2)}) async-start(f32[8,96,256]{2,1,0:T(8,128)} %pad_maximum_fusion), calls=%async_computation.1 | async-start | bytes 1572864 | tf_op jit(solution)/shard_map/all_to_all | solution.py:16
  32.2 0.0 copy-done.1
  32.3 0.0 copy-done
  32.3 1.1 copy.16.residual
  33.5 0.7 compare_convert_fusion.spread
  34.2 9.7 %all-to-all-done.1 = f32[8,96,256]{2,1,0:T(8,128)S(1)} async-done(((f32[8,96,256]{2,1,0:T(8,128)}), f32[8,96,256]{2,1,0:T(8,128)S(1)}, u32[]{:S(2)}, u32[]{:S(2)}) %all-to-all-start.1) | async-done | bytes 786464 | tf_op jit(solution)/shard_map/all_to_all | solution.py:16
  43.8 0.5 copy.24
  44.3 0.9 slice.20.row_gains
  45.2 0.7 slice.21.col_gains
  45.9 35.1 %gradients.1 = (f32[64,8,256]{2,1,0:T(8,128)}, f32[32,8,256]{2,1,0:T(8,128)}) custom-call(f32[64,8,256]{2,1,0:T(8,128)} %slice.20.row_gains, f32[32,8,256]{2,1,0:T(8,128)} %slice.21.col_gains, bf16[64,8,256]{2,1,0:T(8,128)(2,1)} %copy.16.residual, bf16[64,32,8,256]{3,2,1,0:T(8,128)(2,1)} %bitcast.24, bf16[64,32,8,256]{3,2,1,0:T(8,128)(2,1)} %swap.1.turned, ...), custom_call_target="tpu_custom_call" | custom-call | tf_op jit(solution)/shard_map/gradients/pallas_call | solution.py:201
  81.0 1.2 maximum_bitcast_fusion
  82.2 0.3 copy.17
  82.5 15.5 %all_to_all.20 = f32[8,96,256]{2,1,0:T(8,128)S(1)} all-to-all(f32[8,96,256]{2,1,0:T(8,128)S(1)} %copy.17), channel_id=1, replica_groups=mesh['row'=8,'col'=16] {'row'}, dimensions={0} | all-to-all | bytes 1572864 | tf_op jit(solution)/shard_map/all_to_all | solution.py:16
  98.1 1.1 fusion
  99.2 0.1 reshape.96
  99.4 21.9 %all_to_all.21 = f32[128,4,256]{2,1,0:T(4,128)S(1)} all-to-all(f32[128,4,256]{2,1,0:T(4,128)S(1)} %reshape.96), channel_id=1, replica_groups=mesh['row'=8,'col'=16] {'row','col'}, dimensions={0} | all-to-all | bytes 1048576 | tf_op jit(solution)/shard_map/all_to_all | solution.py:16
  121.3 0.1 bitcast_reduce_fusion
  121.3 0.6 copy.18
  (12 shorter events, 0.2 us)
Async XLA Ops:
  1.7 25.1 %all-to-all-start = ((f32[128,4,256]{2,1,0:T(4,128)}), f32[128,4,256]{2,1,0:T(4,128)S(1)}, u32[]{:S(2)}, u32[]{:S(2)}) async-start(f32[128,4,256]{2,1,0:T(4,128)} %bitcast.1), calls=%async_computation | async-start | bytes 1048576 | tf_op jit(solution)/shard_map/all_to_all | solution.py:16
  13.9 13.1 %copy-start.2 = (s32[512]{0:T(512)S(1)}, s32[512]{0:T(512)}, u32[]{:S(2)}) copy-start(s32[512]{0:T(512)} %param.9) | copy-start | bytes 6148
  13.9 18.4 %copy-start.1 = (s32[64,32,1]{0,2,1:T(1,128)S(1)}, s32[64,32,1]{0,2,1:T(1,128)}, u32[]{:S(2)}) copy-start(s32[64,32,1]{0,2,1:T(1,128)} %param.8) | copy-start | bytes 24580
  13.9 18.4 %copy-start = (bf16[64,32,8,1,8]{0,4,3,2,1:T(8,128)(2,1)S(1)}, bf16[64,32,8,1,8]{0,4,3,2,1:T(8,128)(2,1)}, u32[]{:S(2)}) copy-start(bf16[64,32,8,1,8]{0,4,3,2,1:T(8,128)(2,1)} %param.7) | copy-start | bytes 786436
  28.7 15.2 %all-to-all-start.1 = ((f32[8,96,256]{2,1,0:T(8,128)}), f32[8,96,256]{2,1,0:T(8,128)S(1)}, u32[]{:S(2)}, u32[]{:S(2)}) async-start(f32[8,96,256]{2,1,0:T(8,128)} %pad_maximum_fusion), calls=%async_computation.1 | async-start | bytes 1572864 | tf_op jit(solution)/shard_map/all_to_all | solution.py:16

commit v4 on v3

--- a/solution.py
+++ b/solution.py
@@ -9,6 +9,7 @@
 
 LANES = 128
 PER_STEP = 8
+SWAP_STEP = 16
 BATCH = 8
 
 
@@ -43,10 +44,10 @@
     part = jnp.arange(width, dtype=jnp.int32)
     partner = part + jnp.where(part // group % 2 == 0, group, -group)
     swap = (part[:, None] == partner[None, :]).astype(coherency.dtype)
-    block = pl.BlockSpec((PER_STEP, cols, channels, width), lambda s: (s, 0, 0, 0))
+    block = pl.BlockSpec((SWAP_STEP, cols, channels, width), lambda s: (s, 0, 0, 0))
     return pl.pallas_call(
         swap_kernel,
-        grid=(rows // PER_STEP,),
+        grid=(rows // SWAP_STEP,),
         in_specs=[block, pl.BlockSpec((width, width), lambda s: (0, 0))],
         out_specs=block,
         out_shape=jax.ShapeDtypeStruct(coherency.shape, coherency.dtype),
@@ -60,16 +61,15 @@
 
 
 def gradients_kernel(
-    row_gains,
-    col_gains,
+    gains,
     residual,
     coherency,
     turned,
     spread,
-    row_side,
-    col_side,
-    row_parts,
-    row_sums,
+    sides,
+    parts_even,
+    parts_odd,
+    sums_odd,
     col_parts,
     col_sums,
     weights_even,
@@ -79,46 +79,55 @@
 ):
     step = pl.program_id(0)
     per_step, col_count, channels, _ = coherency.shape
-    row_count = row_gains.shape[0]
+    row_count = residual.shape[0]
     lane = lax.broadcasted_iota(jnp.int32, (channels, LANES), 1)
     index = lane // group
     even = index % 2 == 0
     sign = jnp.where(even, -1.0, 1.0).astype(jnp.float32)
 
+    def spread_out(row, weights):
+        weights[...] = lax.dot_general(
+            residual[row],
+            spread[...],
+            (((0,), (0,)), ((), ())),
+            preferred_element_type=jnp.float32,
+        )
+
+    def prepare_row(row, parts):
+        for b in (0, 1):
+            own = gains[row, :, b * LANES : (b + 1) * LANES]
+            for n in range(4):
+                copies = replicas(own, group, index == n)
+                parts[4 * b + n] = copies if n % 2 == 0 else sign * copies
+
+    def finish_row(row, sums):
+        for a in (0, 1):
+            joined = None
+            for n in range(4):
+                own = sums[4 * a + n]
+                part = summed_groups(own if n % 2 == 0 else sign * own, group)
+                joined = part if n == 0 else jnp.where(index == n, part, joined)
+            sides[row, :, a * LANES : (a + 1) * LANES] = joined
+
     @pl.when(step == 0)
     def _():
         col_sums[...] = jnp.zeros(col_sums.shape, col_sums.dtype)
+        sums_odd[...] = jnp.zeros(sums_odd.shape, sums_odd.dtype)
+        spread_out(0, weights_even)
+        prepare_row(0, parts_even)
 
         def prepare_cols(block, carry):
             for j in range(BATCH):
                 k = block * BATCH + j
                 for b in (0, 1):
-                    own = col_gains[k, :, b * LANES : (b + 1) * LANES]
+                    own = gains[row_count + k, :, b * LANES : (b + 1) * LANES]
                     col_parts[k, b] = own
                     col_parts[k, 2 + b] = sign * swapped(own, group, even)
             return carry
 
         lax.fori_loop(0, col_count // BATCH, prepare_cols, 0)
 
-        def prepare_rows(block, carry):
-            for j in range(BATCH):
-                i = block * BATCH + j
-                for b in (0, 1):
-                    own = row_gains[i, :, b * LANES : (b + 1) * LANES]
-                    for n in range(4):
-                        copies = replicas(own, group, index == n)
-                        row_parts[i, 4 * b + n] = copies if n % 2 == 0 else sign * copies
-            return carry
-
-        lax.fori_loop(0, row_count // BATCH, prepare_rows, 0)
-
-    def spread_out(i, weights):
-        weights[...] = lax.dot_general(
-            residual[i], spread[...], (((0,), (0,)), ((), ())), preferred_element_type=jnp.float32
-        )
-
-    def one_row(i, weights):
-        row = step * per_step + i
+    def one_row(i, weights, parts):
         zero = jnp.zeros((channels, LANES), jnp.float32)
         sums = [zero] * 8
         for k in range(col_count):
@@ -140,83 +149,72 @@
                     sums[to] = sums[to] + product * m[c]
                     sums[to + 1] = sums[to + 1] + product * sm[c]
             t = [
-                row_parts[row, 4 * b] * m[0]
-                + row_parts[row, 4 * b + 1] * sm[0]
-                + row_parts[row, 4 * b + 2] * m[1]
-                + row_parts[row, 4 * b + 3] * sm[1]
+                parts[4 * b] * m[0]
+                + parts[4 * b + 1] * sm[0]
+                + parts[4 * b + 2] * m[1]
+                + parts[4 * b + 3] * sm[1]
                 for b in (0, 1)
             ]
             for a in (0, 1):
                 col_sums[k, a] += g[2 * a] * t[0] + g[4 + 2 * a] * t[1]
                 col_sums[k, 2 + a] += g[2 * a + 1] * t[0] + g[4 + 2 * a + 1] * t[1]
-        for n in range(8):
-            row_sums[row, n] = sums[n]
-
-    spread_out(0, weights_even)
+        return sums
 
     def two_rows(half, carry):
         i = 2 * half
-        spread_out(i + 1, weights_odd)
-        one_row(i, weights_even)
-        spread_out(jnp.minimum(i + 2, per_step - 1), weights_even)
-        one_row(i + 1, weights_odd)
+        row = step * per_step + i
+        following = jnp.minimum(row + 2, row_count - 1)
+        finish_row(jnp.maximum(row - 1, 0), sums_odd)
+        spread_out(row + 1, weights_odd)
+        prepare_row(row + 1, parts_odd)
+        finish_row(row, one_row(i, weights_even, parts_even))
+        spread_out(following, weights_even)
+        prepare_row(following, parts_even)
+        sums = one_row(i + 1, weights_odd, parts_odd)
+        for n in range(8):
+            sums_odd[n] = sums[n]
         return carry
 
     lax.fori_loop(0, per_step // 2, two_rows, 0)
 
     @pl.when(step == pl.num_programs(0) - 1)
     def _():
-        def finish_rows(block, carry):
-            for j in range(BATCH):
-                i = block * BATCH + j
-                for a in (0, 1):
-                    joined = None
-                    for n in range(4):
-                        own = row_sums[i, 4 * a + n]
-                        part = summed_groups(own if n % 2 == 0 else sign * own, group)
-                        joined = part if n == 0 else jnp.where(index == n, part, joined)
-                    row_side[i, :, a * LANES : (a + 1) * LANES] = joined
-            return carry
-
-        lax.fori_loop(0, row_count // BATCH, finish_rows, 0)
+        finish_row(row_count - 1, sums_odd)
 
         def finish_cols(block, carry):
             for j in range(BATCH):
                 k = block * BATCH + j
                 for a in (0, 1):
                     back = sign * swapped(col_sums[k, 2 + a], group, even)
-                    col_side[k, :, a * LANES : (a + 1) * LANES] = col_sums[k, a] - back
+                    to = slice(a * LANES, (a + 1) * LANES)
+                    sides[row_count + k, :, to] = col_sums[k, a] - back
             return carry
 
         lax.fori_loop(0, col_count // BATCH, finish_cols, 0)
 
 
-def block_gradients(coherency, turned, residual, row_gains, col_gains, interpret=False):
+def block_gradients(coherency, turned, residual, gains, interpret=False):
     rows, cols, channels, width = coherency.shape
     lane = jnp.arange(8 * LANES, dtype=jnp.int32)
     spread = (lane[None, :8] == (lane[:, None] // LANES)).T.astype(jnp.bfloat16)
     block = pl.BlockSpec((PER_STEP, cols, channels, width), lambda s: (s, 0, 0, 0))
-    every_row = pl.BlockSpec((rows, channels, width), lambda s: (0, 0, 0))
-    every_col = pl.BlockSpec((cols, channels, width), lambda s: (0, 0, 0))
+    whole = pl.BlockSpec((rows + cols, channels, width), lambda s: (0, 0, 0))
     return pl.pallas_call(
         functools.partial(gradients_kernel, group=width // 8),
         grid=(rows // PER_STEP,),
         in_specs=[
-            every_row,
-            every_col,
-            pl.BlockSpec((PER_STEP, 8, cols * channels), lambda s: (s, 0, 0)),
+            whole,
+            pl.BlockSpec((rows, 8, cols * channels), lambda s: (0, 0, 0)),
             block,
             block,
             pl.BlockSpec((8, 8 * LANES), lambda s: (0, 0)),
         ],
-        out_specs=[every_row, every_col],
-        out_shape=[
-            jax.ShapeDtypeStruct((rows, channels, width), jnp.float32),
-            jax.ShapeDtypeStruct((cols, channels, width), jnp.float32),
-        ],
+        out_specs=whole,
+        out_shape=jax.ShapeDtypeStruct((rows + cols, channels, width), jnp.float32),
         scratch_shapes=[
-            pltpu.VMEM((rows, 8, channels, LANES), jnp.float32),
-            pltpu.VMEM((rows, 8, channels, LANES), jnp.float32),
+            pltpu.VMEM((8, channels, LANES), jnp.float32),
+            pltpu.VMEM((8, channels, LANES), jnp.float32),
+            pltpu.VMEM((8, channels, LANES), jnp.float32),
             pltpu.VMEM((cols, 4, channels, LANES), jnp.float32),
             pltpu.VMEM((cols, 4, channels, LANES), jnp.float32),
             pltpu.VMEM((cols * channels, 8 * LANES), jnp.float32),
@@ -225,7 +223,7 @@
         compiler_params=pltpu.CompilerParams(dimension_semantics=("arbitrary",)),
         interpret=interpret,
         name="gradients",
-    )(row_gains, col_gains, residual, coherency, turned, spread)
+    )(gains, residual, coherency, turned, spread)
 
 
 def weighted(cotangent, flags):
@@ -271,15 +269,9 @@
     needed = exchanged(jnp.concatenate([of_rows, of_cols], axis=1), "row")
     by_slot = jnp.transpose(needed, (1, 0, 2))
 
-    row_side, col_side = block_gradients(
-        models,
-        turned,
-        weighted(cotangent, flags),
-        by_slot[:rows],
-        by_slot[rows:],
-    )
-
-    both = jnp.transpose(jnp.concatenate([row_side, col_side], axis=0), (1, 0, 2))
+    sides = block_gradients(models, turned, weighted(cotangent, flags), by_slot)
+
+    both = jnp.transpose(sides, (1, 0, 2))
     arrived = exchanged(both, "row")
     of_slots = arrived[:, :rows].reshape(stations, width)
     col_sum = jnp.sum(arrived[:, rows:], axis=0)

time: 122 us -> 111 us (0.910)
  Pallas kernels: 45.6 us -> 35 us
  waiting for transfers between devices: 12.1 us -> 14.3 us
  blocking collectives: 37.4 us -> 35.2 us
    pallas_call x1, Pallas kernels: 35.1 us -> 26.7 us  [block_gradients(): pl.pallas_call(functools.partial(gradients_kernel, group=width // 8), gri...]
    all_to_all x2, blocking collectives: 37.4 us -> 35.2 us  [exchanged(): return lax.all_to_all(x, axis, split_axis=0, concat_axis=0, tiled=True)]
    pallas_call x1, Pallas kernels: 10.4 us -> 8.26 us  [swapped_pairs(): pl.pallas_call(swap_kernel, grid=(rows // SWAP_STEP,), in_specs=[block, p...]
    all_to_all x2, waiting for transfers between devices: 12.1 us -> 14.3 us  [exchanged(): return lax.all_to_all(x, axis, split_axis=0, concat_axis=0, tiled=True)]
    slice x2 -> x0, local copies, waits for them, and re-layouts: 1.6 us -> none  [the longest x1 0.88 us: shards(): by_slot[:rows]]
  transfers between devices with their start and end apart: 2 -> 2, of which waited for: 2 -> 2; matrix products, arithmetic and copies ran while one was open for 2% -> 2% of each run, Pallas kernels for 9% -> 7%
where the time goes in v4:
time: 111 us
  blocking collectives  35.2 us (32%)
  Pallas kernels  35 us (32%)
  starting transfers between devices  15 us (14%)
  waiting for transfers between devices  14.3 us (13%)
  local copies, waits for them, and re-layouts  6.68 us (6%)
  other arithmetic  2.5 us (2%)
  matrix products  1.8 us (2%)
    all_to_all x2, blocking collectives, exchanged(): return lax.all_to_all(x, axis, split_axis=0, concat_axis=0, tiled=True)  35.2 us
    pallas_call x1, Pallas kernels, block_gradients(): pl.pallas_call(functools.partial(gradients_kernel, group=width // 8), gri...  26.7 us
    all_to_all x2, starting transfers between devices, exchanged(): return lax.all_to_all(x, axis, split_axis=0, concat_axis=0, tiled=True)  15 us
    all_to_all x2, waiting for transfers between devices, exchanged(): return lax.all_to_all(x, axis, split_axis=0, concat_axis=0, tiled=True)  14.3 us
    pallas_call x1, Pallas kernels, swapped_pairs(): pl.pallas_call(swap_kernel, grid=(rows // SWAP_STEP,), in_specs=[block, p...  8.26 us
  transfers between devices with their start and end apart: 2, of which 2 were waited for; matrix products, arithmetic and copies ran while one was open for 2% of the time, Pallas kernels for 7%

profile of v4, /device:TPU:1, one launch (start us, length us, event | category | flops | bytes accessed | tf_op | source)
XLA Modules:
  0.0 110.6 jit_solution(12868327782635898144)
XLA Ops:
  0.0 0.8 copy.13
  0.8 0.9 broadcast_in_dim.10
  1.7 11.5 %all-to-all-start = ((f32[128,4,256]{2,1,0:T(4,128)}), f32[128,4,256]{2,1,0:T(4,128)S(1)}, u32[]{:S(2)}, u32[]{:S(2)}) async-start(f32[128,4,256]{2,1,0:T(4,128)} %bitcast.1), calls=%async_computation | async-start | bytes 1048576 | tf_op jit(solution)/shard_map/all_to_all | solution.py:17
  13.2 0.7 fusion.4.swap
  13.9 0.0 copy-start.2
  13.9 0.0 copy-start.1
  13.9 0.0 copy-start
  13.9 8.3 %swap.1.turned = bf16[64,32,8,256]{3,2,1,0:T(8,128)(2,1)} custom-call(bf16[64,32,8,256]{3,2,1,0:T(8,128)(2,1)} %bitcast.22, bf16[256,256]{1,0:T(8,128)(2,1)} %fusion.4.swap), custom_call_target="tpu_custom_call" | custom-call | flops 2147483648 | bytes 16777216 | tf_op jit(solution)/shard_map/swap/pallas_call | solution.py:48
  22.1 4.6 %all-to-all-done = f32[128,4,256]{2,1,0:T(4,128)S(1)} async-done(((f32[128,4,256]{2,1,0:T(4,128)}), f32[128,4,256]{2,1,0:T(4,128)S(1)}, u32[]{:S(2)}, u32[]{:S(2)}) %all-to-all-start) | async-done | bytes 524320 | tf_op jit(solution)/shard_map/all_to_all | solution.py:17
  26.8 0.2 reshape.92
  27.0 0.0 copy-done.2
  27.0 0.7 fusion.1
  27.7 1.0 pad_maximum_fusion
  28.7 3.5 %all-to-all-start.1 = ((f32[8,96,256]{2,1,0:T(8,128)}), f32[8,96,256]{2,1,0:T(8,128)S(1)}, u32[]{:S(2)}, u32[]{:S(2)}) async-start(f32[8,96,256]{2,1,0:T(8,128)} %pad_maximum_fusion), calls=%async_computation.1 | async-start | bytes 1572864 | tf_op jit(solution)/shard_map/all_to_all | solution.py:17
  32.2 0.0 copy-done.1
  32.3 0.0 copy-done
  32.3 1.2 %copy.16.residual = bf16[64,8,256]{2,1,0:T(8,128)(2,1)} copy(bf16[64,8,256]{0,1,2:T(8,128)(2,1)S(1)} %bitcast.28) | data formatting | bytes 524288 | tf_op jit(solution)/shard_map/reshape | solution.py:232
  33.5 0.7 compare_convert_fusion.spread
  34.2 9.6 %all-to-all-done.1 = f32[8,96,256]{2,1,0:T(8,128)S(1)} async-done(((f32[8,96,256]{2,1,0:T(8,128)}), f32[8,96,256]{2,1,0:T(8,128)S(1)}, u32[]{:S(2)}, u32[]{:S(2)}) %all-to-all-start.1) | async-done | bytes 786464 | tf_op jit(solution)/shard_map/all_to_all | solution.py:17
  43.9 1.4 %copy.24 = f32[8,96,256]{2,0,1:T(8,128)} copy(f32[8,96,256]{2,1,0:T(8,128)S(1)} %all-to-all-done.1) | data formatting | bytes 1572864 | tf_op jit(solution)/shard_map/all_to_all | solution.py:17
  45.2 26.7 %gradients.1 = f32[96,8,256]{2,1,0:T(8,128)} custom-call(f32[96,8,256]{2,1,0:T(8,128)} %bitcast.24, bf16[64,8,256]{2,1,0:T(8,128)(2,1)} %copy.16.residual, bf16[64,32,8,256]{3,2,1,0:T(8,128)(2,1)} %bitcast.23, bf16[64,32,8,256]{3,2,1,0:T(8,128)(2,1)} %swap.1.turned, bf16[8,1024]{1,0:T(8,128)(2,1)} %compare_convert_fusion.spread), custom_call_target="tpu_custom_call" | custom-call | tf_op jit(solution)/shard_map/gradients/pallas_call | solution.py:202
  72.0 1.4 %copy.17 = f32[8,96,256]{2,1,0:T(8,128)S(1)} copy(f32[8,96,256]{2,0,1:T(8,128)} %bitcast.25) | data formatting | bytes 1572864 | tf_op jit(solution)/shard_map/transpose | solution.py:274
  73.3 15.5 %all_to_all.20 = f32[8,96,256]{2,1,0:T(8,128)S(1)} all-to-all(f32[8,96,256]{2,1,0:T(8,128)S(1)} %copy.17), channel_id=1, replica_groups=mesh['row'=8,'col'=16] {'row'}, dimensions={0} | all-to-all | bytes 1572864 | tf_op jit(solution)/shard_map/all_to_all | solution.py:17
  89.0 1.1 %fusion = f32[512,256]{1,0:T(8,128)S(1)} fusion(f32[512,256]{1,0:T(8,128)S(1)} %add_dynamic-update-slice_fusion, s32[512]{0:T(512)S(1)} %copy-done.2), kind=kOutput, calls=%fused_computation.1 | convolution fusion | flops 805568512 | bytes 1050624 | tf_op jit(solution)/shard_map/dot_general | solution.py:236
  90.1 0.1 reshape.96
  90.2 19.7 %all_to_all.21 = f32[128,4,256]{2,1,0:T(4,128)S(1)} all-to-all(f32[128,4,256]{2,1,0:T(4,128)S(1)} %reshape.96), channel_id=1, replica_groups=mesh['row'=8,'col'=16] {'row','col'}, dimensions={0} | all-to-all | bytes 1048576 | tf_op jit(solution)/shard_map/all_to_all | solution.py:17
  109.9 0.1 bitcast_reduce_fusion
  110.0 0.6 copy.18
  (12 shorter events, 0.2 us)
Async XLA Ops:
  1.7 25.1 %all-to-all-start = ((f32[128,4,256]{2,1,0:T(4,128)}), f32[128,4,256]{2,1,0:T(4,128)S(1)}, u32[]{:S(2)}, u32[]{:S(2)}) async-start(f32[128,4,256]{2,1,0:T(4,128)} %bitcast.1), calls=%async_computation | async-start | bytes 1048576 | tf_op jit(solution)/shard_map/all_to_all | solution.py:17
  13.9 13.1 %copy-start.2 = (s32[512]{0:T(512)S(1)}, s32[512]{0:T(512)}, u32[]{:S(2)}) copy-start(s32[512]{0:T(512)} %param.9) | copy-start | bytes 6148
  13.9 18.4 %copy-start.1 = (s32[64,32,1]{0,2,1:T(1,128)S(1)}, s32[64,32,1]{0,2,1:T(1,128)}, u32[]{:S(2)}) copy-start(s32[64,32,1]{0,2,1:T(1,128)} %param.8) | copy-start | bytes 24580
  13.9 18.4 %copy-start = (bf16[64,32,8,1,8]{0,4,3,2,1:T(8,128)(2,1)S(1)}, bf16[64,32,8,1,8]{0,4,3,2,1:T(8,128)(2,1)}, u32[]{:S(2)}) copy-start(bf16[64,32,8,1,8]{0,4,3,2,1:T(8,128)(2,1)} %param.7) | copy-start | bytes 786436
  28.7 15.2 %all-to-all-start.1 = ((f32[8,96,256]{2,1,0:T(8,128)}), f32[8,96,256]{2,1,0:T(8,128)S(1)}, u32[]{:S(2)}, u32[]{:S(2)}) async-start(f32[8,96,256]{2,1,0:T(8,128)} %pad_maximum_fusion), calls=%async_computation.1 | async-start | bytes 1572864 | tf_op jit(solution)/shard_map/all_to_all | solution.py:17

commit v5 on v4

--- a/solution.py
+++ b/solution.py
@@ -11,6 +11,7 @@
 PER_STEP = 8
 SWAP_STEP = 16
 BATCH = 8
+VMEM_LIMIT = 24 * 1024 * 1024
 
 
 def exchanged(x, axis):
@@ -51,7 +52,9 @@
         in_specs=[block, pl.BlockSpec((width, width), lambda s: (0, 0))],
         out_specs=block,
         out_shape=jax.ShapeDtypeStruct(coherency.shape, coherency.dtype),
-        compiler_params=pltpu.CompilerParams(dimension_semantics=("arbitrary",)),
+        compiler_params=pltpu.CompilerParams(
+            dimension_semantics=("arbitrary",), vmem_limit_bytes=VMEM_LIMIT
+        ),
         cost_estimate=pl.CostEstimate(
             flops=2 * width * coherency.size, bytes_accessed=4 * coherency.size, transcendentals=0
         ),
@@ -198,16 +201,16 @@
     lane = jnp.arange(8 * LANES, dtype=jnp.int32)
     spread = (lane[None, :8] == (lane[:, None] // LANES)).T.astype(jnp.bfloat16)
     block = pl.BlockSpec((PER_STEP, cols, channels, width), lambda s: (s, 0, 0, 0))
-    whole = pl.BlockSpec((rows + cols, channels, width), lambda s: (0, 0, 0))
+    whole = pl.BlockSpec(memory_space=pltpu.VMEM)
     return pl.pallas_call(
         functools.partial(gradients_kernel, group=width // 8),
         grid=(rows // PER_STEP,),
         in_specs=[
             whole,
-            pl.BlockSpec((rows, 8, cols * channels), lambda s: (0, 0, 0)),
+            whole,
             block,
             block,
-            pl.BlockSpec((8, 8 * LANES), lambda s: (0, 0)),
+            whole,
         ],
         out_specs=whole,
         out_shape=jax.ShapeDtypeStruct((rows + cols, channels, width), jnp.float32),
@@ -220,7 +223,9 @@
             pltpu.VMEM((cols * channels, 8 * LANES), jnp.float32),
             pltpu.VMEM((cols * channels, 8 * LANES), jnp.float32),
         ],
-        compiler_params=pltpu.CompilerParams(dimension_semantics=("arbitrary",)),
+        compiler_params=pltpu.CompilerParams(
+            dimension_semantics=("arbitrary",), vmem_limit_bytes=VMEM_LIMIT
+        ),
         interpret=interpret,
         name="gradients",
     )(gains, residual, coherency, turned, spread)

time: 111 us -> 113 us (1.018)
  local copies, waits for them, and re-layouts: 6.68 us -> 17.2 us
  Pallas kernels: 35 us -> 26.7 us
  other arithmetic: 2.5 us -> 1.24 us
    unnamed x7 -> x15, local copies, waits for them, and re-layouts: 0.02 us -> 13.4 us
    pallas_call x1, Pallas kernels: 8.26 us -> 2.84 us  [swapped_pairs(): pl.pallas_call(swap_kernel, grid=(rows // SWAP_STEP,), in_specs=[block, p...]
    pallas_call x1, Pallas kernels: 26.7 us -> 23.9 us  [block_gradients(): pl.pallas_call(functools.partial(gradients_kernel, group=width // 8), gri...]
    transpose x1, local copies, waits for them, and re-layouts: 1.39 us -> 0.26 us  [shards(): both = jnp.transpose(sides, (1, 0, 2))]
  transfers between devices with their start and end apart: 2 -> 2, of which waited for: 2 -> 2; matrix products, arithmetic and copies ran while one was open for 2% -> 1% of each run, Pallas kernels for 7% -> 3%
where the time goes in v5:
time: 113 us
  blocking collectives  35.8 us (32%)
  Pallas kernels  26.7 us (24%)
  local copies, waits for them, and re-layouts  17.2 us (15%)
  starting transfers between devices  15 us (13%)
  waiting for transfers between devices  15 us (13%)
  matrix products  1.8 us (2%)
  other arithmetic  1.24 us (1%)
    all_to_all x2, blocking collectives, exchanged(): return lax.all_to_all(x, axis, split_axis=0, concat_axis=0, tiled=True)  35.8 us
    pallas_call x1, Pallas kernels, block_gradients(): pl.pallas_call(functools.partial(gradients_kernel, group=width // 8), gri...  23.9 us
    all_to_all x2, starting transfers between devices, exchanged(): return lax.all_to_all(x, axis, split_axis=0, concat_axis=0, tiled=True)  15 us
    all_to_all x2, waiting for transfers between devices, exchanged(): return lax.all_to_all(x, axis, split_axis=0, concat_axis=0, tiled=True)  15 us
    unnamed x15, local copies, waits for them, and re-layouts  13.4 us
    pallas_call x1, Pallas kernels, swapped_pairs(): pl.pallas_call(swap_kernel, grid=(rows // SWAP_STEP,), in_specs=[block, p...  2.84 us
  transfers between devices with their start and end apart: 2, of which 2 were waited for; matrix products, arithmetic and copies ran while one was open for 1% of the time, Pallas kernels for 3%

profile of v5, /device:TPU:1, one launch (start us, length us, event | category | flops | bytes accessed | tf_op | source)
XLA Modules:
  0.0 113.0 jit_solution(12358838173048172592)
XLA Ops:
  0.0 0.8 copy.13
  0.8 0.9 broadcast_in_dim.10
  1.7 11.5 %all-to-all-start = ((f32[128,4,256]{2,1,0:T(4,128)}), f32[128,4,256]{2,1,0:T(4,128)S(1)}, u32[]{:S(2)}, u32[]{:S(2)}) async-start(f32[128,4,256]{2,1,0:T(4,128)} %bitcast.1), calls=%async_computation | async-start | bytes 1048576 | tf_op jit(solution)/shard_map/all_to_all | solution.py:18
  13.2 0.0 copy-start
  13.2 3.4 %copy-done = bf16[64,32,8,1,256]{4,2,3,1,0:T(8,128)(2,1)S(1)} copy-done((bf16[64,32,8,1,256]{4,2,3,1,0:T(8,128)(2,1)S(1)}, bf16[64,32,8,1,256]{4,2,3,1,0:T(8,128)(2,1)}, u32[]{:S(2)}) %copy-start) | copy-done | bytes 8388632
  16.6 0.0 copy-start.6
  16.6 0.0 copy-start.5
  16.6 0.0 copy-start.4
  16.6 2.8 %swap.1.turned = bf16[64,32,8,256]{3,2,1,0:T(8,128)(2,1)S(1)} custom-call(bf16[64,32,8,256]{3,2,1,0:T(8,128)(2,1)S(1)} %bitcast.22, bf16[256,256]{1,0:T(8,128)(2,1)S(1)} %fusion.4.swap), custom_call_target="tpu_custom_call" | custom-call | flops 2147483648 | bytes 16777216 | tf_op jit(solution)/shard_map/swap/pallas_call | solution.py:49
  19.5 0.0 copy-start.2
  19.5 3.2 %copy-done.2 = bf16[64,32,8,256]{3,2,1,0:T(8,128)(2,1)} copy-done((bf16[64,32,8,256]{3,2,1,0:T(8,128)(2,1)}, bf16[64,32,8,256]{3,2,1,0:T(8,128)(2,1)S(1)}, u32[]{:S(2)}) %copy-start.2) | copy-done | bytes 8388632
  22.7 4.1 %all-to-all-done = f32[128,4,256]{2,1,0:T(4,128)S(1)} async-done(((f32[128,4,256]{2,1,0:T(4,128)}), f32[128,4,256]{2,1,0:T(4,128)S(1)}, u32[]{:S(2)}, u32[]{:S(2)}) %all-to-all-start) | async-done | bytes 524320 | tf_op jit(solution)/shard_map/all_to_all | solution.py:18
  26.8 0.2 reshape.92
  26.9 0.0 copy-done.6
  26.9 0.7 fusion.1
  27.7 1.0 pad_maximum_fusion
  28.7 3.5 %all-to-all-start.1 = ((f32[8,96,256]{2,1,0:T(8,128)}), f32[8,96,256]{2,1,0:T(8,128)S(1)}, u32[]{:S(2)}, u32[]{:S(2)}) async-start(f32[8,96,256]{2,1,0:T(8,128)} %pad_maximum_fusion), calls=%async_computation.1 | async-start | bytes 1572864 | tf_op jit(solution)/shard_map/all_to_all | solution.py:18
  32.2 0.0 copy-done.5
  32.3 0.0 copy-done.4
  32.3 0.4 copy.16.residual
  32.8 0.1 compare_convert_fusion.spread
  32.9 11.0 %all-to-all-done.1 = f32[8,96,256]{2,1,0:T(8,128)S(1)} async-done(((f32[8,96,256]{2,1,0:T(8,128)}), f32[8,96,256]{2,1,0:T(8,128)S(1)}, u32[]{:S(2)}, u32[]{:S(2)}) %all-to-all-start.1) | async-done | bytes 786464 | tf_op jit(solution)/shard_map/all_to_all | solution.py:18
  43.8 0.5 copy.24
  44.3 0.0 copy-start.1
  44.3 3.4 %copy-done.1 = bf16[64,32,8,1,256]{4,2,3,1,0:T(8,128)(2,1)S(1)} copy-done((bf16[64,32,8,1,256]{4,2,3,1,0:T(8,128)(2,1)S(1)}, bf16[64,32,8,1,256]{4,2,3,1,0:T(8,128)(2,1)}, u32[]{:S(2)}) %copy-start.1) | copy-done | bytes 8388632
  47.7 0.0 copy-start.3
  47.7 3.4 %copy-done.3 = bf16[64,32,8,256]{3,2,1,0:T(8,128)(2,1)S(1)} copy-done((bf16[64,32,8,256]{3,2,1,0:T(8,128)(2,1)S(1)}, bf16[64,32,8,256]{3,2,1,0:T(8,128)(2,1)}, u32[]{:S(2)}) %copy-start.3) | copy-done | bytes 8388632
  51.1 23.9 %gradients.1 = f32[96,8,256]{2,1,0:T(8,128)S(1)} custom-call(f32[96,8,256]{2,1,0:T(8,128)S(1)} %bitcast.24, bf16[64,8,256]{2,1,0:T(8,128)(2,1)S(1)} %copy.16.residual, bf16[64,32,8,256]{3,2,1,0:T(8,128)(2,1)S(1)} %bitcast.23, bf16[64,32,8,256]{3,2,1,0:T(8,128)(2,1)S(1)} %copy-done.3, bf16[8,1024]{1,0:T(8,128)(2,1)S(1)} %compare_convert_fusion.spread), custom_call_target="tpu_custom_call" | custom-call | tf_op jit(solution)/shard_map/gradients/pallas_call | solution.py:205
  74.9 0.3 copy.17
  75.2 15.6 %all_to_all.20 = f32[8,96,256]{2,1,0:T(8,128)S(1)} all-to-all(f32[8,96,256]{2,1,0:T(8,128)S(1)} %copy.17), channel_id=1, replica_groups=mesh['row'=8,'col'=16] {'row'}, dimensions={0} | all-to-all | bytes 1572864 | tf_op jit(solution)/shard_map/all_to_all | solution.py:18
  90.8 1.1 fusion
  92.0 0.1 reshape.96
  92.1 20.2 %all_to_all.21 = f32[128,4,256]{2,1,0:T(4,128)S(1)} all-to-all(f32[128,4,256]{2,1,0:T(4,128)S(1)} %reshape.96), channel_id=1, replica_groups=mesh['row'=8,'col'=16] {'row','col'}, dimensions={0} | all-to-all | bytes 1048576 | tf_op jit(solution)/shard_map/all_to_all | solution.py:18
  112.4 0.1 bitcast_reduce_fusion
  112.4 0.6 copy.18
  (13 shorter events, 0.2 us)
Async XLA Ops:
  1.7 25.1 %all-to-all-start = ((f32[128,4,256]{2,1,0:T(4,128)}), f32[128,4,256]{2,1,0:T(4,128)S(1)}, u32[]{:S(2)}, u32[]{:S(2)}) async-start(f32[128,4,256]{2,1,0:T(4,128)} %bitcast.1), calls=%async_computation | async-start | bytes 1048576 | tf_op jit(solution)/shard_map/all_to_all | solution.py:18
  13.2 3.4 %copy-start = (bf16[64,32,8,1,256]{4,2,3,1,0:T(8,128)(2,1)S(1)}, bf16[64,32,8,1,256]{4,2,3,1,0:T(8,128)(2,1)}, u32[]{:S(2)}) copy-start(bf16[64,32,8,1,256]{4,2,3,1,0:T(8,128)(2,1)} %param.6) | copy-start | bytes 25165828
  16.6 10.3 %copy-start.6 = (s32[512]{0:T(512)S(1)}, s32[512]{0:T(512)}, u32[]{:S(2)}) copy-start(s32[512]{0:T(512)} %param.9) | copy-start | bytes 6148
  16.6 15.6 %copy-start.5 = (s32[64,32,1]{0,2,1:T(1,128)S(1)}, s32[64,32,1]{0,2,1:T(1,128)}, u32[]{:S(2)}) copy-start(s32[64,32,1]{0,2,1:T(1,128)} %param.8) | copy-start | bytes 24580
  16.6 15.7 %copy-start.4 = (bf16[64,32,8,1,8]{0,4,3,2,1:T(8,128)(2,1)S(1)}, bf16[64,32,8,1,8]{0,4,3,2,1:T(8,128)(2,1)}, u32[]{:S(2)}) copy-start(bf16[64,32,8,1,8]{0,4,3,2,1:T(8,128)(2,1)} %param.7) | copy-start | bytes 786436
  19.5 3.2 %copy-start.2 = (bf16[64,32,8,256]{3,2,1,0:T(8,128)(2,1)}, bf16[64,32,8,256]{3,2,1,0:T(8,128)(2,1)S(1)}, u32[]{:S(2)}) copy-start(bf16[64,32,8,256]{3,2,1,0:T(8,128)(2,1)S(1)} %swap.1.turned) | copy-start | bytes 25165828
  28.7 15.2 %all-to-all-start.1 = ((f32[8,96,256]{2,1,0:T(8,128)}), f32[8,96,256]{2,1,0:T(8,128)S(1)}, u32[]{:S(2)}, u32[]{:S(2)}) async-start(f32[8,96,256]{2,1,0:T(8,128)} %pad_maximum_fusion), calls=%async_computation.1 | async-start | bytes 1572864 | tf_op jit(solution)/shard_map/all_to_all | solution.py:18
  44.3 3.4 %copy-start.1 = (bf16[64,32,8,1,256]{4,2,3,1,0:T(8,128)(2,1)S(1)}, bf16[64,32,8,1,256]{4,2,3,1,0:T(8,128)(2,1)}, u32[]{:S(2)}) copy-start(bf16[64,32,8,1,256]{4,2,3,1,0:T(8,128)(2,1)} %param.6) | copy-start | bytes 25165828
  47.7 3.4 %copy-start.3 = (bf16[64,32,8,256]{3,2,1,0:T(8,128)(2,1)S(1)}, bf16[64,32,8,256]{3,2,1,0:T(8,128)(2,1)}, u32[]{:S(2)}) copy-start(bf16[64,32,8,256]{3,2,1,0:T(8,128)(2,1)} %copy-done.2) | copy-start | bytes 25165828

commit v6 on v4

--- a/solution.py
+++ b/solution.py
@@ -8,9 +8,10 @@
 from jax.sharding import PartitionSpec as P
 
 LANES = 128
-PER_STEP = 8
+PER_STEP = 4
 SWAP_STEP = 16
 BATCH = 8
+VMEM_LIMIT = 48 * 1024 * 1024
 
 
 def exchanged(x, axis):
@@ -74,12 +75,26 @@
     col_sums,
     weights_even,
     weights_odd,
+    model_slots,
+    turned_slots,
+    arrivals,
     *,
     group,
 ):
-    step = pl.program_id(0)
-    per_step, col_count, channels, _ = coherency.shape
-    row_count = residual.shape[0]
+    row_count, col_count, channels, _ = coherency.shape
+    steps = row_count // PER_STEP
+
+    def fetches(step, slot):
+        rows = pl.ds(step * PER_STEP, PER_STEP)
+        return (
+            pltpu.make_async_copy(coherency.at[rows], model_slots.at[slot], arrivals.at[0, slot]),
+            pltpu.make_async_copy(turned.at[rows], turned_slots.at[slot], arrivals.at[1, slot]),
+        )
+
+    for ahead in (0, 1):
+        for fetch in fetches(ahead, ahead):
+            fetch.start()
+
     lane = lax.broadcasted_iota(jnp.int32, (channels, LANES), 1)
     index = lane // group
     even = index % 2 == 0
@@ -109,31 +124,29 @@
                 joined = part if n == 0 else jnp.where(index == n, part, joined)
             sides[row, :, a * LANES : (a + 1) * LANES] = joined
 
-    @pl.when(step == 0)
-    def _():
-        col_sums[...] = jnp.zeros(col_sums.shape, col_sums.dtype)
-        sums_odd[...] = jnp.zeros(sums_odd.shape, sums_odd.dtype)
-        spread_out(0, weights_even)
-        prepare_row(0, parts_even)
-
-        def prepare_cols(block, carry):
-            for j in range(BATCH):
-                k = block * BATCH + j
-                for b in (0, 1):
-                    own = gains[row_count + k, :, b * LANES : (b + 1) * LANES]
-                    col_parts[k, b] = own
-                    col_parts[k, 2 + b] = sign * swapped(own, group, even)
-            return carry
-
-        lax.fori_loop(0, col_count // BATCH, prepare_cols, 0)
-
-    def one_row(i, weights, parts):
+    col_sums[...] = jnp.zeros(col_sums.shape, col_sums.dtype)
+    sums_odd[...] = jnp.zeros(sums_odd.shape, sums_odd.dtype)
+    spread_out(0, weights_even)
+    prepare_row(0, parts_even)
+
+    def prepare_cols(block, carry):
+        for j in range(BATCH):
+            k = block * BATCH + j
+            for b in (0, 1):
+                own = gains[row_count + k, :, b * LANES : (b + 1) * LANES]
+                col_parts[k, b] = own
+                col_parts[k, 2 + b] = sign * swapped(own, group, even)
+        return carry
+
+    lax.fori_loop(0, col_count // BATCH, prepare_cols, 0)
+
+    def one_row(slot, i, weights, parts):
         zero = jnp.zeros((channels, LANES), jnp.float32)
         sums = [zero] * 8
         for k in range(col_count):
             at = slice(k * channels, (k + 1) * channels)
-            model = coherency[i, k].astype(jnp.float32)
-            other = turned[i, k].astype(jnp.float32)
+            model = model_slots[slot, i, k].astype(jnp.float32)
+            other = turned_slots[slot, i, k].astype(jnp.float32)
             m = [model[:, :LANES], model[:, LANES:]]
             sm = [other[:, :LANES], other[:, LANES:]]
             g = [weights[at, n * LANES : (n + 1) * LANES] for n in range(8)]
@@ -160,54 +173,64 @@
                 col_sums[k, 2 + a] += g[2 * a + 1] * t[0] + g[4 + 2 * a + 1] * t[1]
         return sums
 
-    def two_rows(half, carry):
-        i = 2 * half
-        row = step * per_step + i
-        following = jnp.minimum(row + 2, row_count - 1)
-        finish_row(jnp.maximum(row - 1, 0), sums_odd)
-        spread_out(row + 1, weights_odd)
-        prepare_row(row + 1, parts_odd)
-        finish_row(row, one_row(i, weights_even, parts_even))
-        spread_out(following, weights_even)
-        prepare_row(following, parts_even)
-        sums = one_row(i + 1, weights_odd, parts_odd)
-        for n in range(8):
-            sums_odd[n] = sums[n]
+    def one_step(step, carry):
+        slot = step % 2
+        for fetch in fetches(step, slot):
+            fetch.wait()
+
+        def two_rows(half, inner):
+            i = 2 * half
+            row = step * PER_STEP + i
+            following = jnp.minimum(row + 2, row_count - 1)
+            finish_row(jnp.maximum(row - 1, 0), sums_odd)
+            spread_out(row + 1, weights_odd)
+            prepare_row(row + 1, parts_odd)
+            finish_row(row, one_row(slot, i, weights_even, parts_even))
+            spread_out(following, weights_even)
+            prepare_row(following, parts_even)
+            sums = one_row(slot, i + 1, weights_odd, parts_odd)
+            for n in range(8):
+                sums_odd[n] = sums[n]
+            return inner
+
+        lax.fori_loop(0, PER_STEP // 2, two_rows, 0)
+
+        @pl.when(step + 2 < steps)
+        def _():
+            for fetch in fetches(step + 2, slot):
+                fetch.start()
+
         return carry
 
-    lax.fori_loop(0, per_step // 2, two_rows, 0)
-
-    @pl.when(step == pl.num_programs(0) - 1)
-    def _():
-        finish_row(row_count - 1, sums_odd)
-
-        def finish_cols(block, carry):
-            for j in range(BATCH):
-                k = block * BATCH + j
-                for a in (0, 1):
-                    back = sign * swapped(col_sums[k, 2 + a], group, even)
-                    to = slice(a * LANES, (a + 1) * LANES)
-                    sides[row_count + k, :, to] = col_sums[k, a] - back
-            return carry
-
-        lax.fori_loop(0, col_count // BATCH, finish_cols, 0)
+    lax.fori_loop(0, steps, one_step, 0)
+    finish_row(row_count - 1, sums_odd)
+
+    def finish_cols(block, carry):
+        for j in range(BATCH):
+            k = block * BATCH + j
+            for a in (0, 1):
+                back = sign * swapped(col_sums[k, 2 + a], group, even)
+                sides[row_count + k, :, a * LANES : (a + 1) * LANES] = col_sums[k, a] - back
+        return carry
+
+    lax.fori_loop(0, col_count // BATCH, finish_cols, 0)
 
 
 def block_gradients(coherency, turned, residual, gains, interpret=False):
     rows, cols, channels, width = coherency.shape
     lane = jnp.arange(8 * LANES, dtype=jnp.int32)
     spread = (lane[None, :8] == (lane[:, None] // LANES)).T.astype(jnp.bfloat16)
-    block = pl.BlockSpec((PER_STEP, cols, channels, width), lambda s: (s, 0, 0, 0))
-    whole = pl.BlockSpec((rows + cols, channels, width), lambda s: (0, 0, 0))
+    in_hbm = pl.BlockSpec(memory_space=pltpu.HBM)
+    slots = pltpu.VMEM((2, PER_STEP, cols, channels, width), coherency.dtype)
+    whole = pl.BlockSpec(memory_space=pltpu.VMEM)
     return pl.pallas_call(
         functools.partial(gradients_kernel, group=width // 8),
-        grid=(rows // PER_STEP,),
         in_specs=[
             whole,
-            pl.BlockSpec((rows, 8, cols * channels), lambda s: (0, 0, 0)),
-            block,
-            block,
-            pl.BlockSpec((8, 8 * LANES), lambda s: (0, 0)),
+            whole,
+            in_hbm,
+            in_hbm,
+            whole,
         ],
         out_specs=whole,
         out_shape=jax.ShapeDtypeStruct((rows + cols, channels, width), jnp.float32),
@@ -219,8 +242,11 @@
             pltpu.VMEM((cols, 4, channels, LANES), jnp.float32),
             pltpu.VMEM((cols * channels, 8 * LANES), jnp.float32),
             pltpu.VMEM((cols * channels, 8 * LANES), jnp.float32),
+            slots,
+            slots,
+            pltpu.SemaphoreType.DMA((2, 2)),
         ],
-        compiler_params=pltpu.CompilerParams(dimension_semantics=("arbitrary",)),
+        compiler_params=pltpu.CompilerParams(vmem_limit_bytes=VMEM_LIMIT),
         interpret=interpret,
         name="gradients",
     )(gains, residual, coherency, turned, spread)

time: 111 us -> 106 us (0.955)
  Pallas kernels: 35 us -> 32 us
  local copies, waits for them, and re-layouts: 6.68 us -> 3.88 us
  waiting for transfers between devices: 14.3 us -> 15.6 us
    pallas_call x1, Pallas kernels: 26.7 us -> 23.8 us  [block_gradients(): pl.pallas_call(functools.partial(gradients_kernel, group=width // 8), in_...]
    all_to_all x2, waiting for transfers between devices: 14.3 us -> 15.6 us  [exchanged(): return lax.all_to_all(x, axis, split_axis=0, concat_axis=0, tiled=True)]
    transpose x1, local copies, waits for them, and re-layouts: 1.39 us -> 0.26 us  [shards(): both = jnp.transpose(sides, (1, 0, 2))]
  transfers between devices with their start and end apart: 2 -> 2, of which waited for: 2 -> 2; matrix products, arithmetic and copies ran while one was open for 2% -> 1% of each run, Pallas kernels for 7% -> 8%
where the time goes in v6:
time: 106 us
  blocking collectives  35.5 us (33%)
  Pallas kernels  32 us (30%)
  waiting for transfers between devices  15.6 us (15%)
  starting transfers between devices  15 us (14%)
  local copies, waits for them, and re-layouts  3.88 us (4%)
  other arithmetic  1.89 us (2%)
  matrix products  1.8 us (2%)
    all_to_all x2, blocking collectives, exchanged(): return lax.all_to_all(x, axis, split_axis=0, concat_axis=0, tiled=True)  35.5 us
    pallas_call x1, Pallas kernels, block_gradients(): pl.pallas_call(functools.partial(gradients_kernel, group=width // 8), in_...  23.8 us
    all_to_all x2, waiting for transfers between devices, exchanged(): return lax.all_to_all(x, axis, split_axis=0, concat_axis=0, tiled=True)  15.6 us
    all_to_all x2, starting transfers between devices, exchanged(): return lax.all_to_all(x, axis, split_axis=0, concat_axis=0, tiled=True)  15 us
    pallas_call x1, Pallas kernels, swapped_pairs(): pl.pallas_call(swap_kernel, grid=(rows // SWAP_STEP,), in_specs=[block, p...  8.26 us
  transfers between devices with their start and end apart: 2, of which 2 were waited for; matrix products, arithmetic and copies ran while one was open for 1% of the time, Pallas kernels for 8%

profile of v6, /device:TPU:1, one launch (start us, length us, event | category | flops | bytes accessed | tf_op | source)
XLA Modules:
  0.0 105.9 jit_solution(4910131469213782186)
XLA Ops:
  0.0 0.8 copy.13
  0.8 0.9 broadcast_in_dim.10
  1.7 11.5 %all-to-all-start = ((f32[128,4,256]{2,1,0:T(4,128)}), f32[128,4,256]{2,1,0:T(4,128)S(1)}, u32[]{:S(2)}, u32[]{:S(2)}) async-start(f32[128,4,256]{2,1,0:T(4,128)} %bitcast.1), calls=%async_computation | async-start | bytes 1048576 | tf_op jit(solution)/shard_map/all_to_all | solution.py:18
  13.2 0.7 fusion.4.swap
  13.9 0.0 copy-start.2
  13.9 0.0 copy-start.1
  13.9 0.0 copy-start
  13.9 8.3 %swap.1.turned = bf16[64,32,8,256]{3,2,1,0:T(8,128)(2,1)} custom-call(bf16[64,32,8,256]{3,2,1,0:T(8,128)(2,1)} %bitcast.24, bf16[256,256]{1,0:T(8,128)(2,1)} %fusion.4.swap), custom_call_target="tpu_custom_call" | custom-call | flops 2147483648 | bytes 16777216 | tf_op jit(solution)/shard_map/swap/pallas_call | solution.py:49
  22.1 4.6 %all-to-all-done = f32[128,4,256]{2,1,0:T(4,128)S(1)} async-done(((f32[128,4,256]{2,1,0:T(4,128)}), f32[128,4,256]{2,1,0:T(4,128)S(1)}, u32[]{:S(2)}, u32[]{:S(2)}) %all-to-all-start) | async-done | bytes 524320 | tf_op jit(solution)/shard_map/all_to_all | solution.py:18
  26.8 0.2 reshape.92
  27.0 0.0 copy-done.2
  27.0 0.7 fusion.1
  27.7 1.0 pad_maximum_fusion
  28.7 3.5 %all-to-all-start.1 = ((f32[8,96,256]{2,1,0:T(8,128)}), f32[8,96,256]{2,1,0:T(8,128)S(1)}, u32[]{:S(2)}, u32[]{:S(2)}) async-start(f32[8,96,256]{2,1,0:T(8,128)} %pad_maximum_fusion), calls=%async_computation.1 | async-start | bytes 1572864 | tf_op jit(solution)/shard_map/all_to_all | solution.py:18
  32.2 0.0 copy-done.1
  32.3 0.0 copy-done
  32.3 0.4 copy.16.residual
  32.8 0.1 compare_convert_fusion.spread
  32.9 11.0 %all-to-all-done.1 = f32[8,96,256]{2,1,0:T(8,128)S(1)} async-done(((f32[8,96,256]{2,1,0:T(8,128)}), f32[8,96,256]{2,1,0:T(8,128)S(1)}, u32[]{:S(2)}, u32[]{:S(2)}) %all-to-all-start.1) | async-done | bytes 786464 | tf_op jit(solution)/shard_map/all_to_all | solution.py:18
  43.9 0.5 copy.24
  44.3 23.8 %gradients.1 = f32[96,8,256]{2,1,0:T(8,128)S(1)} custom-call(f32[96,8,256]{2,1,0:T(8,128)S(1)} %bitcast.22, bf16[64,8,256]{2,1,0:T(8,128)(2,1)S(1)} %copy.16.residual, bf16[64,32,8,256]{3,2,1,0:T(8,128)(2,1)} %bitcast.25, bf16[64,32,8,256]{3,2,1,0:T(8,128)(2,1)} %swap.1.turned, bf16[8,1024]{1,0:T(8,128)(2,1)S(1)} %compare_convert_fusion.spread), custom_call_target="tpu_custom_call" | custom-call | tf_op jit(solution)/shard_map/gradients/pallas_call | solution.py:226
  68.1 0.3 copy.17
  68.3 15.2 %all_to_all.20 = f32[8,96,256]{2,1,0:T(8,128)S(1)} all-to-all(f32[8,96,256]{2,1,0:T(8,128)S(1)} %copy.17), channel_id=1, replica_groups=mesh['row'=8,'col'=16] {'row'}, dimensions={0} | all-to-all | bytes 1572864 | tf_op jit(solution)/shard_map/all_to_all | solution.py:18
  83.6 1.1 %fusion = f32[512,256]{1,0:T(8,128)S(1)} fusion(f32[512,256]{1,0:T(8,128)S(1)} %add_dynamic-update-slice_fusion, s32[512]{0:T(512)S(1)} %copy-done.2), kind=kOutput, calls=%fused_computation.1 | convolution fusion | flops 805568512 | bytes 1050624 | tf_op jit(solution)/shard_map/dot_general | solution.py:262
  84.7 0.1 reshape.96
  84.9 20.3 %all_to_all.21 = f32[128,4,256]{2,1,0:T(4,128)S(1)} all-to-all(f32[128,4,256]{2,1,0:T(4,128)S(1)} %reshape.96), channel_id=1, replica_groups=mesh['row'=8,'col'=16] {'row','col'}, dimensions={0} | all-to-all | bytes 1048576 | tf_op jit(solution)/shard_map/all_to_all | solution.py:18
  105.2 0.1 bitcast_reduce_fusion
  105.2 0.6 copy.18
  (12 shorter events, 0.2 us)
Async XLA Ops:
  1.7 25.1 %all-to-all-start = ((f32[128,4,256]{2,1,0:T(4,128)}), f32[128,4,256]{2,1,0:T(4,128)S(1)}, u32[]{:S(2)}, u32[]{:S(2)}) async-start(f32[128,4,256]{2,1,0:T(4,128)} %bitcast.1), calls=%async_computation | async-start | bytes 1048576 | tf_op jit(solution)/shard_map/all_to_all | solution.py:18
  13.9 13.1 %copy-start.2 = (s32[512]{0:T(512)S(1)}, s32[512]{0:T(512)}, u32[]{:S(2)}) copy-start(s32[512]{0:T(512)} %param.9) | copy-start | bytes 6148
  13.9 18.4 %copy-start.1 = (s32[64,32,1]{0,2,1:T(1,128)S(1)}, s32[64,32,1]{0,2,1:T(1,128)}, u32[]{:S(2)}) copy-start(s32[64,32,1]{0,2,1:T(1,128)} %param.8) | copy-start | bytes 24580
  13.9 18.4 %copy-start = (bf16[64,32,8,1,8]{0,4,3,2,1:T(8,128)(2,1)S(1)}, bf16[64,32,8,1,8]{0,4,3,2,1:T(8,128)(2,1)}, u32[]{:S(2)}) copy-start(bf16[64,32,8,1,8]{0,4,3,2,1:T(8,128)(2,1)} %param.7) | copy-start | bytes 786436
  28.7 15.2 %all-to-all-start.1 = ((f32[8,96,256]{2,1,0:T(8,128)}), f32[8,96,256]{2,1,0:T(8,128)S(1)}, u32[]{:S(2)}, u32[]{:S(2)}) async-start(f32[8,96,256]{2,1,0:T(8,128)} %pad_maximum_fusion), calls=%async_computation.1 | async-start | bytes 1572864 | tf_op jit(solution)/shard_map/all_to_all | solution.py:18
